TPU v7x, 8 devices: a whole 2x2x1 slice. The times are simulated.
8 devices in a mesh: data: 4 (over z, y, x), stage: 2 (over core).
Axes of the slice: x: 2, y: 2, z: 1, core: 2. Of those that a mesh axis runs over, the one named last changes fastest.
Arguments:
- w_first: float32 [2, 512, 2048], P('stage')
- w_second: float32 [2, 2048, 512], P('stage')
- mom_first: float32 [2, 512, 2048], P('stage')
- mom_second: float32 [2, 2048, 512], P('stage')
- vel_first: float32 [2, 512, 2048], P('stage')
- vel_second: float32 [2, 2048, 512], P('stage')
- grad_first: float32 [2, 512, 2048], P('stage')
- grad_second: float32 [2, 2048, 512], P('stage')
- embed_table: float32 [32128, 512], replicated
- mom_embed: float32 [32128, 512], replicated
- vel_embed: float32 [32128, 512], replicated
- grad_embed: float32 [32128, 512], replicated
- stage_acts: bfloat16 [2, 4096, 512], P('stage', 'data')
- last_tokens: int32 [4096], P('data')
- targets: int32 [4096], P('data')
- next_tokens: int32 [16, 4096], P(None, 'data')
- max_norm: float32 [1], replicated
Outputs:
- output 1: float32 [2, 512, 2048], P('stage')
- output 2: float32 [2, 2048, 512], P('stage')
- output 3: float32 [2, 512, 2048], P('stage')
- output 4: float32 [2, 2048, 512], P('stage')
- output 5: float32 [2, 512, 2048], P('stage')
- output 6: float32 [2, 2048, 512], P('stage')
- output 7: float32 [32128, 512], replicated
- output 8: float32 [32128, 512], replicated
- output 9: float32 [32128, 512], replicated
- output 10: bfloat16 [16, 4096, 512], P(None, 'data')
All inputs are finite; a program needn't handle non-finite values.
Results may differ from a plain program's by a relative error of at most 0.00534546.
Values are sent between devices in bfloat16 or wider.
A program may use at most 2.25 GiB of HBM per device.

v0:
```python
import math
import jax
import jax.numpy as jnp
from jax import lax
from jax.sharding import PartitionSpec as P

STEP_COUNT = 10
LEARN_RATE = 1e-3
ADAM_BETA1 = 0.9
ADAM_BETA2 = 0.95
ADAM_EPS = 1e-8
WEIGHT_DECAY = 0.1
CLIP_EPS = 1e-6


def block_forward(act_in, w_in, w_out):
    pre_act = jnp.dot(act_in, w_in, preferred_element_type=jnp.float32)
    hidden = jax.nn.gelu(pre_act).astype(jnp.bfloat16)
    mlp_out = jnp.dot(hidden, w_out, preferred_element_type=jnp.float32)
    return (act_in.astype(jnp.float32) + mlp_out).astype(jnp.bfloat16)


def block_backward(d_out, act_in, w_in, w_out):
    pre_act = jnp.dot(act_in, w_in, preferred_element_type=jnp.float32)
    hidden, gelu_back = jax.vjp(jax.nn.gelu, pre_act)
    grad_out = jnp.einsum('tf,td->fd', hidden.astype(jnp.bfloat16), d_out, preferred_element_type=jnp.float32)
    d_hidden = jnp.einsum('td,fd->tf', d_out, w_out, preferred_element_type=jnp.float32)
    d_pre = gelu_back(d_hidden)[0].astype(jnp.bfloat16)
    grad_in = jnp.einsum('td,tf->df', act_in, d_pre, preferred_element_type=jnp.float32)
    d_back = jnp.einsum('tf,df->td', d_pre, w_in, preferred_element_type=jnp.float32)
    d_act = (d_out.astype(jnp.float32) + d_back).astype(jnp.bfloat16)
    return d_act, grad_in, grad_out


def head_backward(top_out, table_b, targets):
    logits = jnp.einsum('td,vd->tv', top_out, table_b, preferred_element_type=jnp.float32)
    soft_probs = jax.nn.softmax(logits, axis=-1)
    is_target = jnp.arange(table_b.shape[0])[None, :] == targets[:, None]
    d_logits = jnp.where(is_target, soft_probs - 1.0, soft_probs).astype(jnp.bfloat16)
    d_top = jnp.dot(d_logits, table_b, preferred_element_type=jnp.float32).astype(jnp.bfloat16)
    head_grad = jnp.einsum('tv,td->vd', d_logits, top_out, preferred_element_type=jnp.float32)
    return d_top, head_grad


def adamw_update(master, moment, velocity, gradient, clip_scale):
    scaled_grad = clip_scale * gradient
    moment_new = ADAM_BETA1 * moment + (1.0 - ADAM_BETA1) * scaled_grad
    velocity_new = ADAM_BETA2 * velocity + (1.0 - ADAM_BETA2) * scaled_grad * scaled_grad
    moment_hat = moment_new / (1.0 - ADAM_BETA1 ** STEP_COUNT)
    velocity_hat = velocity_new / (1.0 - ADAM_BETA2 ** STEP_COUNT)
    master_new = master - LEARN_RATE * (moment_hat / (jnp.sqrt(velocity_hat) + ADAM_EPS) + WEIGHT_DECAY * master)
    return master_new, moment_new, velocity_new


def solution(mesh):
    n_stage = mesh.shape['stage']
    n_rep = mesh.shape['data']
    down_pairs = [(j, j - 1) for j in range(1, n_stage)]
    up_pairs = [(j, j + 1) for j in range(n_stage - 1)]
    w_spec = P('stage', None, None)
    in_specs = (w_spec,) * 8 + (P(None, None),) * 4 + (P('stage', 'data', None), P('data'), P('data'), P(None, 'data'), P(None))
    out_specs = (w_spec,) * 6 + (P(None, None),) * 3 + (P(None, 'data', None),)

    def local_step(w_first, w_second, mom_first, mom_second, vel_first, vel_second, grad_first, grad_second,
                   embed_table, mom_embed, vel_embed, grad_embed, stage_acts, last_tokens, targets, next_tokens, max_norm):
        stage_id = lax.axis_index('stage')
        is_last = stage_id == n_stage - 1
        vocab, d_model = embed_table.shape
        scale_in = math.sqrt(d_model)
        w_in = w_first[0].astype(jnp.bfloat16)
        w_out = w_second[0].astype(jnp.bfloat16)
        table_b = embed_table.astype(jnp.bfloat16)
        act_in = stage_acts[0]

        def with_head(top_in):
            return head_backward(block_forward(top_in, w_in, w_out), table_b, targets)

        def without_head(top_in):
            return jnp.zeros_like(top_in), jnp.zeros((vocab, d_model), jnp.float32)

        d_top, head_grad = lax.cond(is_last, with_head, without_head, act_in)

        def back_step(step_idx, loop_state):
            d_in, sum_in, sum_out, d_keep = loop_state
            active = stage_id == n_stage - 1 - step_idx

            def work(operands):
                return block_backward(operands[0], act_in, w_in, w_out)

            def rest(operands):
                return jnp.zeros_like(operands[0]), operands[1], operands[2]

            d_act, sum_in, sum_out = lax.cond(active, work, rest, (d_in, sum_in, sum_out))
            d_keep = jnp.where(active, d_act, d_keep)
            d_in = lax.ppermute(d_act, 'stage', down_pairs)
            return d_in, sum_in, sum_out, d_keep

        init_state = (d_top, jnp.zeros(w_in.shape, jnp.float32), jnp.zeros(w_out.shape, jnp.float32), jnp.zeros_like(act_in))
        _, step_in, step_out, d_own = lax.fori_loop(0, n_stage, back_step, init_state)
        d_low = jnp.where(stage_id == 0, d_own, jnp.zeros_like(d_own))
        low_grad = scale_in * jax.ops.segment_sum(d_low.astype(jnp.float32), last_tokens, num_segments=vocab)

        full_first = grad_first[0] + lax.psum(step_in, 'data') / n_rep
        full_second = grad_second[0] + lax.psum(step_out, 'data') / n_rep
        full_embed = grad_embed + lax.psum(head_grad + low_grad, ('data', 'stage')) / n_rep
        stage_sq = jnp.sum(full_first * full_first) + jnp.sum(full_second * full_second)
        total_sq = lax.psum(stage_sq, 'stage') + jnp.sum(full_embed * full_embed)
        clip_scale = jnp.minimum(1.0, max_norm[0] / (jnp.sqrt(total_sq) + CLIP_EPS))
        new_first, new_mom_first, new_vel_first = adamw_update(w_first[0], mom_first[0], vel_first[0], full_first, clip_scale)
        new_second, new_mom_second, new_vel_second = adamw_update(w_second[0], mom_second[0], vel_second[0], full_second, clip_scale)
        new_embed, new_mom_embed, new_vel_embed = adamw_update(embed_table, mom_embed, vel_embed, full_embed, clip_scale)

        next_in = new_first.astype(jnp.bfloat16)
        next_out = new_second.astype(jnp.bfloat16)
        next_table = new_embed.astype(jnp.bfloat16)
        n_micro, tokens = next_tokens.shape
        start_act = (scale_in * jnp.take(next_table, next_tokens.reshape(-1), axis=0).astype(jnp.float32)).astype(jnp.bfloat16)

        def run_block(carry_act):
            return block_forward(carry_act, next_in, next_out)

        def keep_block(carry_act):
            return carry_act

        def fwd_step(step_idx, carry_act):
            carry_act = lax.cond(stage_id == step_idx, run_block, keep_block, carry_act)
            return lax.ppermute(carry_act, 'stage', up_pairs)

        carry_act = lax.fori_loop(0, n_stage - 1, fwd_step, start_act)
        final_act = lax.cond(is_last, run_block, keep_block, carry_act)
        gathered_out = lax.psum(jnp.where(is_last, final_act, jnp.zeros_like(final_act)), 'stage')
        next_acts = gathered_out.reshape(n_micro, tokens, d_model)
        return (new_first[None], new_second[None], new_mom_first[None], new_mom_second[None],
                new_vel_first[None], new_vel_second[None], new_embed, new_mom_embed, new_vel_embed, next_acts)

    return jax.shard_map(local_step, mesh=mesh, in_specs=in_specs, out_specs=out_specs, check_vma=False)
```

profile of v0, /device:TPU:0, one launch (start us, length us, event | category | flops | bytes accessed | tf_op | source)
XLA Modules:
  0.0 2169.8 jit_solution(14197170537079979980)
XLA Ops:
  7.3 2.6 bitcast_convert_fusion
  9.9 0.8 copy-done.2
  10.7 1.8 bitcast_convert_fusion.1
  12.5 31.8 %convert_element_type.91 = bf16[32128,512]{1,0:T(8,128)(2,1)} convert(f32[32128,512]{1,0:T(8,128)} %param.35) | non-fusion elementwise | flops 16449536 | bytes 98697216 | tf_op jit(solution)/shard_map/convert_element_type | solution.py:72
  44.4 30.2 %conditional.4 = (bf16[1024,512]{1,0:T(8,128)(2,1)}, f32[32128,512]{1,0:T(8,128)}) conditional(s32[]{:T(128)} %convert_element_type.88, () %tuple.53, (s32[1024]{0:T(1024)S(1)}, bf16[1024,512]{1,0:T(8,128)(2,1)S(1)}, bf16[512,2048]{1,0:T(8,128)(2,1)}, bf16[2048,512]{1,0:T(8,128)(2,1)S(1)}, bf16[32128,512]{1,0:T(8,128)(2,1)}) %tuple.113), branch_computations={%region_0.0_spmd, %region_1.4_spmd} | conditional | flops 105677979648 | bytes 737435648 | solution.py:81
  44.4 21.3 broadcast.100
  65.7 1.1 broadcast.99
  74.6 2.5 broadcast_in_dim.44
  77.2 2.5 broadcast_in_dim.45
  79.7 303.8 %while.15 = (s32[]{:T(128)}, bf16[1024,512]{1,0:T(8,128)(2,1)}, f32[512,2048]{0,1:T(8,128)}, f32[2048,512]{1,0:T(8,128)}, bf16[1024,512]{1,0:T(8,128)(2,1)S(1)},...) while((s32[]{:T(128)}, bf16[1024,512]{1,0:T(8,128)(2,1)}, ...), condition=%wide.region_7.8_spmd.clone, body=%wide.region_4.7_spmd.clone.sunk | while | flops 10800857088 | bytes 82837824 | solution.py:99
  79.8 1.3 collective-permute-start
  81.1 0.4 select_select_fusion.2
  81.5 270.7 %collective-permute-done = bf16[1024,512]{1,0:T(8,128)(2,1)} collective-permute-done((bf16[1024,512]{1,0:T(8,128)(2,1)S(1)}, bf16[1024,512]{1,0:T(8,128)(2,1)}, u32[]{:S(2)}, u32[]{:S(2)}) %collective-permute-start) | collective-permute-done | bytes 1048608 | tf_op jit(solution)/shard_map/while/body/eval_jaxpr/ppermute | solution.py:95
  352.2 26.9 %conditional.9 = (bf16[1024,512]{1,0:T(8,128)(2,1)S(1)}, f32[512,2048]{0,1:T(8,128)}, f32[2048,512]{1,0:T(8,128)}) conditional(s32[]{:T(128)} %convert_element_type.138, (f32[512,2048]{0,1:T(8,128)}, f32[2048,512]{1,0:T(8,128)}) %tuple.87, (bf16[1024,512]{1,0:T(8,128)(2,1)}, bf16[2048,512]{1,0:T(8,128)(2,1)}, bf16[1024,512]{1,0:T(8,128)(2,1)S(1)}, ...), branch_computations={%region_5.5_spmd, %region_6.6_spmd} | conditional | flops 10799808512 | bytes 75497552 | solution.py:93
  352.2 4.1 fusion.84
  356.3 8.8 fusion.26
  365.1 3.6 add_convert_fusion.1
  368.7 4.5 convolution_bitcast_fusion
  373.2 5.9 fusion.27
  379.1 1.3 collective-permute-start
  380.8 2.8 collective-permute-done
  383.6 5.3 copy.28
  388.9 0.4 all-reduce.5.cloned.1.call-start
  389.4 1.5 select_convert_fusion
  390.8 21.3 broadcast.126
  412.1 121.2 %scatter_fusion = f32[32128,512]{1,0:T(8,128)} fusion(f32[32128,512]{1,0:T(8,128)} %broadcast.126, s32[1024]{0:T(1024)S(1)} %copy-done.19, f32[1024,512]{1,0:T(8,128)S(1)} %copy-done.6), kind=kCustom, calls=%fused_computation.1 | custom fusion | flops 524288 | bytes 6295552 | tf_op jit(solution)/shard_map/scatter-add | solution.py:101
  533.3 63.0 %multiply_add_fusion.2 = f32[32128,512]{1,0:T(8,128)} fusion(f32[32128,512]{1,0:T(8,128)} %get-tuple-element.256, f32[32128,512]{1,0:T(8,128)} %scatter_fusion), kind=kLoop, calls=%fused_computation.80 | loop fusion | flops 32899072 | bytes 197394432 | tf_op jit(solution)/shard_map/add | solution.py:105
  596.4 0.8 copy-done.16
  597.3 0.6 compare_and_fusion
  598.0 0.6 broadcast_clamp_fusion
  598.6 7.4 multiply_reduce_fusion.1
  606.0 3.7 multiply_reduce_fusion.2
  611.6 3.2 psum.37
  614.8 716.8 %all-reduce.5.cloned.1.call-done = f32[32128,512]{1,0:T(8,128)} async-done(((f32[32128,512]{1,0:T(8,128)}), f32[32128,512]{1,0:T(8,128)}) %all-reduce.5.cloned.1.call-update) | async-done | bytes 65798160 | tf_op jit(solution)/shard_map/psum | solution.py:105
  1331.6 40.4 %multiply_reduce_fusion = f32[]{:T(128)} fusion(f32[32128,512]{1,0:T(8,128)} %param.38, f32[32128,512]{1,0:T(8,128)} %all-reduce.5.cloned.1.call-done), kind=kLoop, calls=%fused_computation.78 | loop fusion | flops 65798144 | bytes 131596288 | tf_op jit(solution)/shard_map/reduce_sum | solution.py:107
  1373.4 176.1 %fusion.81 = (bf16[32128,512]{1,0:T(8,128)(2,1)}, f32[32128,512]{1,0:T(8,128)}, f32[32128,512]{1,0:T(8,128)}, f32[32128,512]{1,0:T(8,128)}) fusion(f32[32128,512]{1,0:T(8,128)} %param.35, f32[32128,512]{1,0:T(8,128)} %param.38, f32[32128,512]{1,0:T(8,128)} %all-reduce.5.cloned.1.call-done, f32[]{:T(128)S(6)} %min.3, f32[32128,512]{1,0:T(8,128)} %param.36, ...), kind=kLoop, calls=%fused_computation.114 | loop fusion | flops 312541184 | bytes 559284224 | tf_op jit(solution)/shard_map/convert_element_type | solution.py:115
  1549.5 266.4 %gather_fusion = bf16[16384,512]{1,0:T(8,128)(2,1)} fusion(bf16[32128,512]{1,0:T(8,128)(2,1)} %get-tuple-element.317, s32[16384]{0:T(1024)S(1)} %copy-done.15), kind=kCustom, calls=%fused_computation | custom fusion | bytes 33619968 | tf_op jit(solution)/shard_map/jit(_take)/gather | solution.py:117
  1816.0 17.3 multiply_convert_fusion.2
  1833.3 8.6 fusion.79
  1841.9 10.9 fusion.80
  1852.9 103.9 %conditional.5 = (bf16[16384,512]{1,0:T(8,128)(2,1)}) conditional(s32[]{:T(128)} %convert_element_type.93, bf16[16384,512]{1,0:T(8,128)(2,1)} %multiply_convert_fusion.2, (bf16[16384,512]{1,0:T(8,128)(2,1)}, bf16[512,2048]{1,0:T(8,128)(2,1)}, bf16[2048,512]{1,0:T(8,128)(2,1)S(1)}) %tuple.110), branch_computations={%region_16.17_spmd, %region_17.18_spmd} | conditional | flops 69046632448 | bytes 71303176 | solution.py:126
  1852.9 13.7 copy.68
  1866.6 90.0 %add_convert_fusion.2 = bf16[16384,512]{1,0:T(8,128)(2,1)} fusion(bf16[16384,512]{1,0:T(8,128)(2,1)} %copy.68, bf16[2048,512]{1,0:T(8,128)(2,1)S(1)} %get-tuple-element.234, bf16[512,2048]{1,0:T(8,128)(2,1)} %get-tuple-element.233), kind=kOutput, calls=%fused_computation.51 | convolution fusion | flops 69046632448 | bytes 37748736 | tf_op jit(solution)/shard_map/while/body/eval_jaxpr/cond/branch_1_fun/dot_general | solution.py:19
  1956.8 7.0 collective-permute-start.1
  1963.8 19.0 collective-permute-done.1
  1982.8 6.5 broadcast_select_fusion
  1989.4 159.9 %all-reduce.7.cloned.1.call-done = bf16[16,1024,512]{2,1,0:T(8,128)(2,1)} async-done(((bf16[16,1024,512]{2,1,0:T(8,128)(2,1)}), bf16[16,1024,512]{2,1,0:T(8,128)(2,1)}) %all-reduce.7.cloned.1.call-update) | async-done | bytes 16777232 | tf_op jit(solution)/shard_map/psum | solution.py:131
  2149.3 13.8 copy.70
  (54 shorter events, 0.9 us)
Async XLA Ops:
  7.2 591.4 %all-reduce.9.cloned.1.call-start = ((), (), s32[]{:S(2)}) async-start(), calls=%async_computation.2 | async-start | bytes 16777216 | tf_op jit(solution)/shard_map/psum | solution.py:103
  7.2 3.5 copy-start.2
  10.7 33.7 %copy-start.11 = (bf16[2048,512]{1,0:T(8,128)(2,1)}, bf16[2048,512]{1,0:T(8,128)(2,1)S(1)}, u32[]{:S(2)}) copy-start(bf16[2048,512]{1,0:T(8,128)(2,1)S(1)} %bitcast_convert_fusion) | copy-start | bytes 6291460
  12.5 31.9 %copy-start.18 = (s32[1024]{0:T(1024)S(1)}, s32[1024]{0:T(1024)}, u32[]{:S(2)}) copy-start(s32[1024]{0:T(1024)} %param.41) | copy-start | bytes 12292
  12.5 31.9 %copy-start.20 = (bf16[1,1024,512]{2,1,0:T(8,128)(2,1)S(1)}, bf16[1,1024,512]{2,1,0:T(8,128)(2,1)}, u32[]{:S(2)}) copy-start(bf16[1,1024,512]{2,1,0:T(8,128)(2,1)} %param.39) | copy-start | bytes 3145732
  74.6 5.1 copy-start
  79.8 272.4 %collective-permute-start = (bf16[1024,512]{1,0:T(8,128)(2,1)S(1)}, bf16[1024,512]{1,0:T(8,128)(2,1)}, u32[]{:S(2)}, u32[]{:S(2)}) collective-permute-start(bf16[1024,512]{1,0:T(8,128)(2,1)S(1)} %get-tuple-element.389), channel_id=1, source_target_pairs={{1,0},{3,2},{5,4},{7,6}} | collective-permute-start | bytes 3145736 | tf_op jit(solution)/shard_map/while/body/eval_jaxpr/ppermute | solution.py:95
  352.2 4.1 copy-start.12
  356.3 8.8 copy-start.13
  379.1 4.5 collective-permute-start
  388.9 942.7 %all-reduce.5.cloned.1.call-start = ((), (), s32[]{:S(2)}) async-start(), calls=%async_computation | async-start | bytes 131596288 | tf_op jit(solution)/shard_map/psum | solution.py:105
  390.8 21.3 copy-start.6
  390.8 21.3 copy-start.19
  596.3 0.8 copy-start.16
  596.4 1552.9 %all-reduce.7.cloned.1.call-start = ((), (), s32[]{:S(2)}) async-start(), calls=%async_computation.1 | async-start | bytes 33554432 | tf_op jit(solution)/shard_map/psum | solution.py:131
  598.6 7.4 copy-start.9
  598.6 7.4 copy-start.10
  1373.4 176.1 %copy-start.15 = (s32[16384]{0:T(1024)S(1)}, s32[16384]{0:T(1024)}, u32[]{:S(2)}) copy-start(s32[16384]{0:T(1024)} %broadcast_clamp_fusion) | copy-start | bytes 196612
  1549.5 266.5 %copy-start.17 = (pred[16384]{0:T(1024)(128)(4,1)S(1)}, pred[16384]{0:T(1024)(128)(4,1)}, u32[]{:S(2)}) copy-start(pred[16384]{0:T(1024)(128)(4,1)} %compare_and_fusion) | copy-start | bytes 49156
  1815.9 17.4 copy-start.1
  1815.9 17.4 copy-start.5
  1816.0 17.4 copy-start.7
  1816.0 17.3 copy-start.8
  1833.3 8.6 copy-start.3
  1833.3 8.6 copy-start.4
  1841.9 11.0 copy-start.14
  1956.8 26.1 %collective-permute-start.1 = (bf16[16384,512]{1,0:T(8,128)(2,1)}, bf16[16384,512]{1,0:T(8,128)(2,1)}, u32[]{:S(2)}, u32[]{:S(2)}) collective-permute-start(bf16[16384,512]{1,0:T(8,128)(2,1)} %get-tuple-element.447), channel_id=1, source_target_pairs={{0,1},{2,3},{4,5},{6,7}} | collective-permute-start | bytes 50331656 | tf_op jit(solution)/shard_map/while/body/eval_jaxpr/ppermute | solution.py:127
Sparse Core Ops, SparseCore 0:
  389.0 162.1 all-reduce.8
  596.5 735.0 all-reduce.4
  1989.5 159.7 all-reduce.6
where the time goes:
time: 2190 us; the launch traced here: 2170 us
  waiting for transfers between devices  1170 us (53%)
  other arithmetic  495 us (23%)
  local copies, waits for them, and re-layouts  350 us (16%)
  matrix products  117 us (5%)
    psum x1, waiting for transfers between devices, local_step(): lax.psum(head_grad + low_grad, ('data', 'stage')) / n_rep  717 us
    ppermute x2, waiting for transfers between devices, back_step(): d_in = lax.ppermute(d_act, 'stage', down_pairs)  273 us
    gather x1, local copies, waits for them, and re-layouts, local_step(): jnp.take(next_table, next_tokens.reshape(-1), axis=0).astype(jnp.float32)  266 us
    convert_element_type x1, other arithmetic, local_step(): next_table = new_embed.astype(jnp.bfloat16)  176 us
    psum x1, waiting for transfers between devices, local_step(): lax.psum(jnp.where(is_last, final_act, jnp.zeros_like(final_act)), 'stage')  160 us
    scatter-add x1, other arithmetic, local_step(): jax.ops.segment_sum(d_low.astype(jnp.float32), last_tokens, num_segments=...  121 us
    dot_general x1, matrix products, block_forward(): mlp_out = jnp.dot(hidden, w_out, preferred_element_type=jnp.float32)  90 us
    add x1, other arithmetic, local_step(): head_grad + low_grad  63 us
  transfers between devices with their start and end apart: 6, of which 5 were waited for; matrix products, arithmetic and copies ran while one was open for 10% of the time, Pallas kernels for 0%

commit v1 on v0

v1 whole, which is shorter than its diff:
```python
import functools
import math
import jax
import jax.numpy as jnp
from jax import lax
from jax.experimental import pallas as pl
from jax.experimental.pallas import tpu as pltpu
from jax.sharding import PartitionSpec as P

STEP_COUNT = 10
LEARN_RATE = 1e-3
ADAM_BETA1 = 0.9
ADAM_BETA2 = 0.95
ADAM_EPS = 1e-8
WEIGHT_DECAY = 0.1
CLIP_EPS = 1e-6

TILE = 512
ADAM_TILE = 1024
CHUNK = 512
SEG = 128
TOKEN_BLOCK = 512
FF_CHUNK = 512
WIDE_TILES = 5
NEG = -1e30
GELU_K = math.sqrt(2.0 / math.pi)
GELU_A = 0.044715
BOTH = ('data', 'stage')


def block_forward(act_in, w_in, w_out):
    pre_act = jnp.dot(act_in, w_in, preferred_element_type=jnp.float32)
    hidden = jax.nn.gelu(pre_act).astype(jnp.bfloat16)
    mlp_out = jnp.dot(hidden, w_out, preferred_element_type=jnp.float32)
    return (act_in.astype(jnp.float32) + mlp_out).astype(jnp.bfloat16)


def backward_kernel(n_chunks, g_ref, x_ref, wi_ref, wo_ref, dx_ref, dwi_ref, dwo_ref, back_ref, acc_i, acc_o):
    f = pl.program_id(0)
    wi = wi_ref[...]
    wi_flip = wi.T
    acc_i[...] = jnp.zeros_like(acc_i)
    acc_o[...] = jnp.zeros_like(acc_o)

    @pl.when(f == 0)
    def _():
        back_ref[...] = jnp.zeros_like(back_ref)

    def chunk(c, _):
        rows = pl.ds(pl.multiple_of(c * CHUNK, CHUNK), CHUNK)
        x, g = x_ref[rows, :], g_ref[rows, :]
        pre = dot_last(wi_flip, x)
        d_hidden = dot_last(wo_ref[...], g)
        square = pre * pre
        bend = jnp.tanh(GELU_K * pre * (1.0 + GELU_A * square))
        rise = 0.5 * (1.0 + bend)
        hidden = (pre * rise).astype(jnp.bfloat16)
        slope = rise + (0.5 * GELU_K) * pre * (1.0 - bend * bend) * (1.0 + (3.0 * GELU_A) * square)
        d_pre = (d_hidden * slope).astype(jnp.bfloat16)
        acc_o[...] += jnp.dot(hidden, g, preferred_element_type=jnp.float32)
        acc_i[...] += jnp.dot(d_pre, x, preferred_element_type=jnp.float32)
        back_ref[c] += jnp.dot(wi, d_pre, preferred_element_type=jnp.float32)
        return 0

    lax.fori_loop(0, n_chunks, chunk, 0, unroll=2)
    dwo_ref[...] = acc_o[...]
    dwi_ref[...] = acc_i[...].T

    @pl.when(f == pl.num_programs(0) - 1)
    def _():
        def last(c, _):
            rows = pl.ds(pl.multiple_of(c * CHUNK, CHUNK), CHUNK)
            dx_ref[rows, :] = (g_ref[rows, :].astype(jnp.float32) + back_ref[c].T).astype(jnp.bfloat16)
            return 0
        lax.fori_loop(0, n_chunks, last, 0)


def block_backward(d_out, act_in, w_in, w_out):
    n_tok, d_model = act_in.shape
    ff = w_in.shape[1]
    n_chunks = n_tok // CHUNK
    tokens = pl.BlockSpec((n_tok, d_model), lambda f: (0, 0))
    cols = pl.BlockSpec((d_model, FF_CHUNK), lambda f: (0, f))
    rows = pl.BlockSpec((FF_CHUNK, d_model), lambda f: (f, 0))
    return pl.pallas_call(
        functools.partial(backward_kernel, n_chunks),
        out_shape=[jax.ShapeDtypeStruct((n_tok, d_model), jnp.bfloat16), jax.ShapeDtypeStruct((d_model, ff), jnp.float32),
                   jax.ShapeDtypeStruct((ff, d_model), jnp.float32)],
        grid=(ff // FF_CHUNK,),
        in_specs=[tokens, tokens, cols, rows],
        out_specs=[tokens, cols, rows],
        scratch_shapes=[pltpu.VMEM((n_chunks, d_model, CHUNK), jnp.float32), pltpu.VMEM((FF_CHUNK, d_model), jnp.float32),
                        pltpu.VMEM((FF_CHUNK, d_model), jnp.float32)],
        compiler_params=params(),
        cost_estimate=pl.CostEstimate(flops=10 * n_tok * d_model * ff, bytes_accessed=12 * d_model * ff, transcendentals=0),
        name='block_backward',
    )(d_out, act_in, w_in, w_out)


def adamw_update(master, moment, velocity, gradient, clip_scale):
    scaled_grad = clip_scale * gradient
    moment_new = ADAM_BETA1 * moment + (1.0 - ADAM_BETA1) * scaled_grad
    velocity_new = ADAM_BETA2 * velocity + (1.0 - ADAM_BETA2) * scaled_grad * scaled_grad
    moment_hat = moment_new / (1.0 - ADAM_BETA1 ** STEP_COUNT)
    velocity_hat = velocity_new / (1.0 - ADAM_BETA2 ** STEP_COUNT)
    master_new = master - LEARN_RATE * (moment_hat / (jnp.sqrt(velocity_hat) + ADAM_EPS) + WEIGHT_DECAY * master)
    return master_new, moment_new, velocity_new


def dot_last(a, b):
    return lax.dot_general(a, b, (((1,), (1,)), ((), ())), preferred_element_type=jnp.float32)


def params(limit_mib=60, **kw):
    return pltpu.CompilerParams(vmem_limit_bytes=limit_mib * 1024 * 1024, **kw)


def load_rows(block, e_ref, vocab):
    rows = block * TILE + lax.broadcasted_iota(jnp.int32, (TILE, 1), 0)
    valid = rows < vocab
    e_tile = jnp.where(valid, e_ref[...], 0.0).astype(jnp.bfloat16)
    return rows, valid, e_tile, jnp.where(valid, 0.0, NEG)


def tile_of(n_own, blk_ref, j):
    return jnp.where(j < n_own, blk_ref[0] + j, blk_ref[1] + j)


def stats_kernel(vocab, n_chunks, n_own, blk_ref, z_ref, e_ref, stat_ref):
    _, _, e_tile, bias = load_rows(tile_of(n_own, blk_ref, pl.program_id(0)), e_ref, vocab)

    @pl.when(pl.program_id(0) == 0)
    def _():
        stat_ref[0:1, :] = jnp.full((1, stat_ref.shape[1]), NEG, jnp.float32)
        stat_ref[1:2, :] = jnp.zeros((1, stat_ref.shape[1]), jnp.float32)

    def chunk(c, _):
        cols = pl.ds(pl.multiple_of(c * CHUNK, CHUNK), CHUNK)
        logits = dot_last(e_tile, z_ref[cols, :]) + bias
        top_old = stat_ref[0:1, cols]
        top_new = jnp.maximum(top_old, jnp.max(logits, axis=0, keepdims=True))
        part = jnp.sum(jnp.exp(logits - top_new), axis=0, keepdims=True)
        stat_ref[0:1, cols] = top_new
        stat_ref[1:2, cols] = stat_ref[1:2, cols] * jnp.exp(top_old - top_new) + part
        return 0

    lax.fori_loop(0, n_chunks, chunk, 0, unroll=4)


def head_stats(z_all, embed_table, blocks, n_own, n_tiles):
    vocab, d_model = embed_table.shape
    n_tok = z_all.shape[0]
    last = (vocab - 1) // TILE
    return pl.pallas_call(
        functools.partial(stats_kernel, vocab, n_tok // CHUNK, n_own),
        out_shape=jax.ShapeDtypeStruct((2, n_tok), jnp.float32),
        grid_spec=pltpu.PrefetchScalarGridSpec(
            num_scalar_prefetch=1, grid=(n_tiles,),
            in_specs=[pl.BlockSpec((n_tok, d_model), lambda j, b: (0, 0)),
                      pl.BlockSpec((TILE, d_model), lambda j, b: (jnp.minimum(tile_of(n_own, b, j), last), 0))],
            out_specs=pl.BlockSpec((2, n_tok), lambda j, b: (0, 0))),
        compiler_params=params(),
        cost_estimate=pl.CostEstimate(flops=2 * n_tiles * TILE * n_tok * d_model, bytes_accessed=n_tiles * TILE * d_model * 4, transcendentals=0),
        name='head_stats',
    )(blocks, z_all, embed_table)


def head_kernel(vocab, n_chunks, n_rep, n_own, with_top, blk_ref, z_ref, norm_ref, tgt_ref, e_ref, g_ref, out_ref, *rest):
    top_ref = rest[0] if with_top else None
    acc_ref = rest[-1]
    j = pl.program_id(0)
    rows, valid, e_tile, bias = load_rows(tile_of(n_own, blk_ref, j), e_ref, vocab)
    if with_top:
        e_flip = e_tile.T

        @pl.when(j == 0)
        def _():
            top_ref[...] = jnp.zeros_like(top_ref)

    def chunk(with_rows, c, _):
        cols = pl.ds(pl.multiple_of(c * CHUNK, CHUNK), CHUNK)
        z_chunk = z_ref[cols, :]
        logits = dot_last(e_tile, z_chunk) + bias
        probs = jnp.exp(logits - norm_ref[0:1, cols]) * norm_ref[1:2, cols]
        d_logits = jnp.where(rows == tgt_ref[0:1, cols], probs - 1.0, probs).astype(jnp.bfloat16)
        if with_rows:
            acc_ref[...] += jnp.dot(d_logits, z_chunk, preferred_element_type=jnp.float32)
        if with_top:
            top_ref[c] += jnp.dot(e_flip, d_logits, preferred_element_type=jnp.float32)
        return 0

    @pl.when(j < n_own)
    def _():
        acc_ref[...] = jnp.zeros_like(acc_ref)
        lax.fori_loop(0, n_chunks, functools.partial(chunk, True), 0, unroll=2 if with_top else 4)
        out_ref[...] = jnp.where(valid, g_ref[...], 0.0) + acc_ref[...] * (1.0 / n_rep)

    if with_top:
        @pl.when(j >= n_own)
        def _():
            lax.fori_loop(0, n_chunks, functools.partial(chunk, False), 0, unroll=2)


def head_grads(z_all, norm, targets, embed_table, grad_embed, blocks, n_own, n_tiles, n_rep, with_top):
    vocab, d_model = embed_table.shape
    n_tok = z_all.shape[0]
    n_chunks = n_tok // CHUNK
    last = (vocab - 1) // TILE
    out_shape = [jax.ShapeDtypeStruct((n_own * TILE, d_model), jnp.float32)]
    out_specs = [pl.BlockSpec((TILE, d_model), lambda j, b: (jnp.minimum(j, n_own - 1), 0))]
    if with_top:
        out_shape.append(jax.ShapeDtypeStruct((n_chunks, d_model, CHUNK), jnp.float32))
        out_specs.append(pl.BlockSpec((n_chunks, d_model, CHUNK), lambda j, b: (0, 0, 0)))
    return pl.pallas_call(
        functools.partial(head_kernel, vocab, n_chunks, n_rep, n_own, with_top),
        out_shape=out_shape,
        grid_spec=pltpu.PrefetchScalarGridSpec(
            num_scalar_prefetch=1, grid=(n_tiles,),
            in_specs=[pl.BlockSpec((n_tok, d_model), lambda j, b: (0, 0)),
                      pl.BlockSpec((2, n_tok), lambda j, b: (0, 0)),
                      pl.BlockSpec((1, n_tok), lambda j, b: (0, 0)),
                      pl.BlockSpec((TILE, d_model), lambda j, b: (jnp.minimum(tile_of(n_own, b, j), last), 0)),
                      pl.BlockSpec((TILE, d_model), lambda j, b: (jnp.minimum(b[0] + jnp.minimum(j, n_own - 1), last), 0))],
            out_specs=out_specs,
            scratch_shapes=[pltpu.VMEM((TILE, d_model), jnp.float32)]),
        compiler_params=params(),
        cost_estimate=pl.CostEstimate(flops=(6 if with_top else 4) * n_tiles * TILE * n_tok * d_model,
                                      bytes_accessed=n_tiles * TILE * d_model * 12, transcendentals=0),
        name='head_grads' if with_top else 'head_rows',
    )(blocks, z_all, norm, targets, embed_table, grad_embed)


def sparse_rows(block, start_ref, ids_ref, low_ref, base):
    rows = block * TILE + lax.broadcasted_iota(jnp.int32, (TILE, 1), 0)
    first = start_ref[block] // SEG
    stop = (start_ref[block + 1] + SEG - 1) // SEG

    def segment(c, acc):
        pick = jnp.where(rows == ids_ref[pl.ds(c, 1), :], 1.0, 0.0).astype(jnp.bfloat16)
        return acc + jnp.dot(pick, low_ref[pl.ds(pl.multiple_of(c * SEG, SEG), SEG), :], preferred_element_type=jnp.float32)

    return lax.fori_loop(first, stop, segment, base)


def sumsq_kernel(low_scale, blk_ref, start_ref, ids_ref, low_ref, g_ref, out_ref):
    block = blk_ref[0] + pl.program_id(0)
    zero = jnp.zeros(g_ref.shape, jnp.float32)
    full = g_ref[...] + low_scale * sparse_rows(block, start_ref, ids_ref, low_ref, zero)

    @pl.when(pl.program_id(0) == 0)
    def _():
        out_ref[...] = jnp.zeros_like(out_ref)

    out_ref[...] += jnp.sum((full * full).reshape(-1, 8, full.shape[1]), axis=0)


def rows_sumsq(blocks, starts, ids, low, g_rows, n_tiles, low_scale):
    d_model = g_rows.shape[1]
    return pl.pallas_call(
        functools.partial(sumsq_kernel, low_scale),
        out_shape=jax.ShapeDtypeStruct((8, d_model), jnp.float32),
        grid_spec=pltpu.PrefetchScalarGridSpec(
            num_scalar_prefetch=2, grid=(n_tiles,),
            in_specs=[pl.BlockSpec(ids.shape, lambda j, b, s: (0, 0)),
                      pl.BlockSpec(low.shape, lambda j, b, s: (0, 0)),
                      pl.BlockSpec((TILE, d_model), lambda j, b, s: (b[1] + j, 0))],
            out_specs=pl.BlockSpec((8, d_model), lambda j, b, s: (0, 0))),
        compiler_params=params(),
        name='rows_sumsq',
    )(blocks, starts, ids, low, g_rows)


def adam_kernel(low_scale, n_wide, n_red, start_ref, stage_ref, clip_ref, ids_ref, low_ref, gw_ref, go_ref, gf_ref,
                w_ref, m_ref, v_ref, w_out, m_out, v_out, acc_ref):
    j = pl.program_id(0)
    own = n_wide + n_red * stage_ref[0]
    is_own = (j >= own) & (j < own + n_red)

    @pl.when(j < n_wide)
    def _():
        acc_ref[...] = gw_ref[...]

    @pl.when(is_own)
    def _():
        acc_ref[...] = go_ref[...]

    @pl.when((j >= n_wide) & jnp.logical_not(is_own))
    def _():
        acc_ref[...] = gf_ref[...]

    rows = j * ADAM_TILE + lax.broadcasted_iota(jnp.int32, (ADAM_TILE, 1), 0)

    def segment(c, _):
        pick = jnp.where(rows == ids_ref[pl.ds(c, 1), :], 1.0, 0.0).astype(jnp.bfloat16)
        acc_ref[...] += low_scale * jnp.dot(pick, low_ref[pl.ds(pl.multiple_of(c * SEG, SEG), SEG), :], preferred_element_type=jnp.float32)
        return 0

    per = ADAM_TILE // TILE
    lax.fori_loop(start_ref[per * j] // SEG, (start_ref[per * j + per] + SEG - 1) // SEG, segment, 0)

    def part(i, _):
        r = pl.ds(pl.multiple_of(i * 32, 32), 32)
        w_new, m_new, v_new = adamw_update(w_ref[r, :], m_ref[r, :], v_ref[r, :], acc_ref[r, :], clip_ref[0])
        w_out[r, :] = w_new
        m_out[r, :] = m_new
        v_out[r, :] = v_new
        return 0

    lax.fori_loop(0, ADAM_TILE // 32, part, 0)


def embed_adam(starts, stage, clip, ids, low, g_wide, g_own, g_far, embed_table, mom, vel, low_scale):
    vocab, d_model = embed_table.shape
    n_wide, n_red = g_wide.shape[0] // ADAM_TILE, g_own.shape[0] // ADAM_TILE
    spec = pl.BlockSpec((ADAM_TILE, d_model), lambda j, s, t, c: (j, 0))
    shape = jax.ShapeDtypeStruct((vocab, d_model), jnp.float32)

    def held(first):
        return pl.BlockSpec((ADAM_TILE, d_model), lambda j, s, t, c: (jnp.clip(j - n_wide - n_red * first(t[0]), 0, n_red - 1), 0))

    return pl.pallas_call(
        functools.partial(adam_kernel, low_scale, n_wide, n_red),
        out_shape=[shape] * 3,
        grid_spec=pltpu.PrefetchScalarGridSpec(
            num_scalar_prefetch=3, grid=(pl.cdiv(vocab, ADAM_TILE),),
            in_specs=[pl.BlockSpec(ids.shape, lambda j, s, t, c: (0, 0)),
                      pl.BlockSpec(low.shape, lambda j, s, t, c: (0, 0)),
                      pl.BlockSpec((ADAM_TILE, d_model), lambda j, s, t, c: (jnp.minimum(j, n_wide - 1), 0)),
                      held(lambda t: t), held(lambda t: 1 - t), spec, spec, spec],
            out_specs=[spec] * 3,
            scratch_shapes=[pltpu.VMEM((ADAM_TILE, d_model), jnp.float32)]),
        compiler_params=params(),
        cost_estimate=pl.CostEstimate(flops=20 * vocab * d_model, bytes_accessed=28 * vocab * d_model, transcendentals=0),
        name='embed_adam',
    )(starts, stage, clip, ids, low, g_wide, g_own, g_far, embed_table, mom, vel)


def next_kernel(scale, n_blocks, ids_ref, table_ref, wi0_ref, wo0_ref, wi1_ref, wo1_ref, out_ref, rows_ref, x_ref, acc_ref, sems):
    blk = pl.program_id(0)
    slot = lax.rem(blk, 2)
    n_ff = wi0_ref.shape[1] // FF_CHUNK
    per = TOKEN_BLOCK // (2 * n_ff)

    def fetch(base, to_slot, first, count):
        for t in range(count):
            row = ids_ref[base + first + t]
            pltpu.make_async_copy(table_ref.at[pl.ds(row, 1), :], rows_ref.at[to_slot, pl.ds(first + t, 1), :], sems.at[to_slot]).start()

    @pl.when(blk == 0)
    def _():
        def step(i, _):
            fetch(0, 0, i * 16, 16)
            return 0
        lax.fori_loop(0, TOKEN_BLOCK // 16, step, 0)

    pltpu.make_async_copy(rows_ref.at[1 - slot], rows_ref.at[slot], sems.at[slot]).wait()
    base = jnp.minimum(blk + 1, n_blocks - 1) * TOKEN_BLOCK
    more = blk + 1 < n_blocks
    x_ref[...] = (scale * rows_ref[slot].astype(jnp.bfloat16).astype(jnp.float32)).astype(jnp.bfloat16)

    for layer, (wi_ref, wo_ref) in enumerate(((wi0_ref, wo0_ref), (wi1_ref, wo1_ref))):
        acc_ref[...] = x_ref[...].astype(jnp.float32)
        for c in range(n_ff):
            @pl.when(more)
            def _():
                fetch(base, 1 - slot, (layer * n_ff + c) * per, per)
            cols = pl.ds(c * FF_CHUNK, FF_CHUNK)
            pre_act = jnp.dot(x_ref[...], wi_ref[:, cols], preferred_element_type=jnp.float32)
            hidden = jax.nn.gelu(pre_act).astype(jnp.bfloat16)
            acc_ref[...] += jnp.dot(hidden, wo_ref[cols, :], preferred_element_type=jnp.float32)
        if layer == 0:
            x_ref[...] = acc_ref[...].astype(jnp.bfloat16)
        else:
            out_ref[...] = acc_ref[...].astype(jnp.bfloat16)


def next_forward(ids, table, wi0, wo0, wi1, wo1, scale):
    n_tok = ids.shape[0]
    d_model = table.shape[1]
    whole = [pl.BlockSpec(w.shape, lambda j, s: (0, 0)) for w in (wi0, wo0, wi1, wo1)]
    return pl.pallas_call(
        functools.partial(next_kernel, scale, n_tok // TOKEN_BLOCK),
        out_shape=jax.ShapeDtypeStruct((n_tok, d_model), jnp.bfloat16),
        grid_spec=pltpu.PrefetchScalarGridSpec(
            num_scalar_prefetch=1, grid=(n_tok // TOKEN_BLOCK,),
            in_specs=[pl.BlockSpec(memory_space=pl.ANY)] + whole,
            out_specs=pl.BlockSpec((TOKEN_BLOCK, d_model), lambda j, s: (j, 0)),
            scratch_shapes=[pltpu.VMEM((2, TOKEN_BLOCK, d_model), jnp.float32), pltpu.VMEM((TOKEN_BLOCK, d_model), jnp.bfloat16),
                            pltpu.VMEM((TOKEN_BLOCK, d_model), jnp.float32), pltpu.SemaphoreType.DMA((2,))]),
        compiler_params=params(),
        cost_estimate=pl.CostEstimate(flops=8 * n_tok * d_model * wi0.shape[1], bytes_accessed=6 * n_tok * d_model, transcendentals=0),
        name='next_forward',
    )(ids, table, wi0, wo0, wi1, wo1)


def solution(mesh):
    n_stage = mesh.shape['stage']
    n_rep = mesh.shape['data']
    n_dev = n_stage * n_rep
    swap = [(0, 1), (1, 0)]
    w_spec = P('stage', None, None)
    in_specs = (w_spec,) * 8 + (P(None, None),) * 4 + (P('stage', 'data', None), P('data'), P('data'), P(None, 'data'), P(None))
    out_specs = (w_spec,) * 6 + (P(None, None),) * 3 + (P(None, 'data', None),)

    def local_step(w_first, w_second, mom_first, mom_second, vel_first, vel_second, grad_first, grad_second,
                   embed_table, mom_embed, vel_embed, grad_embed, stage_acts, last_tokens, targets, next_tokens, max_norm):
        stage_id = lax.axis_index('stage')
        dev_id = lax.axis_index('data') * n_stage + stage_id
        low_core = stage_id == 0
        vocab, d_model = embed_table.shape
        scale_in = math.sqrt(d_model)
        low_scale = scale_in / n_rep
        n_tiles = -(-vocab // (TILE * n_dev))
        n_wide = WIDE_TILES
        n_rest = n_tiles - n_wide
        n_red = n_rest * n_dev // n_stage
        n_part = n_red // n_rep
        rest0 = n_dev * n_wide

        def other(x):
            return lax.ppermute(x, 'stage', swap)

        def by_stage(own, far):
            return jnp.where(low_core, own, far), jnp.where(low_core, far, own)

        w_in, w_out = w_first[0].astype(jnp.bfloat16), w_second[0].astype(jnp.bfloat16)
        w_in0, w_in1 = by_stage(w_in, other(w_in))
        w_out0, w_out1 = by_stage(w_out, other(w_out))

        z_own = block_forward(stage_acts[0], w_in, w_out)
        cut = z_own.shape[0] // 2
        z_piece = jnp.where(low_core, lax.ppermute(z_own[:cut], 'stage', [(1, 0)]), z_own[cut:])
        all_ids = lax.all_gather(jnp.stack([last_tokens, targets]), 'data', axis=1, tiled=True)
        ids, tgts = all_ids[0], all_ids[1:2]
        n_tok = ids.shape[0]
        half = n_tok // 2
        z_all = lax.all_gather(z_piece, BOTH, axis=0, tiled=True)

        order = jnp.arange(n_tok, dtype=jnp.int32)
        before = (ids[None, :] < ids[:, None]) | ((ids[None, :] == ids[:, None]) & (order[None, :] < order[:, None]))
        rank = jnp.sum(before.astype(jnp.int32), axis=1)
        sorted_ids = jnp.sum(jnp.where(rank[None, :] == order[:, None], ids[None, :], 0), axis=1).reshape(n_tok // SEG, SEG)
        edges = TILE * jnp.arange(n_tiles * n_dev + 1, dtype=jnp.int32)
        starts = jnp.sum((ids[None, :] < edges[:, None]).astype(jnp.int32), axis=1)
        z_all, rank, sorted_ids, starts, acts_in = lax.optimization_barrier((z_all, rank, sorted_ids, starts, stage_acts[0]))

        acts = lax.all_gather(acts_in, 'data', axis=0, tiled=True)
        mine = lax.dynamic_slice_in_dim(acts, stage_id * half, half)
        far = other(lax.dynamic_slice_in_dim(acts, (1 - stage_id) * half, half))
        act0, act1 = by_stage(mine, far)

        def blocks(*tiles):
            return jnp.stack([jnp.asarray(t, jnp.int32) for t in tiles])

        shard = blocks(dev_id * n_wide, rest0 + dev_id * n_rest - n_wide)
        stat = head_stats(z_all, embed_table, shard, n_wide, n_tiles)
        stats = lax.all_gather(stat, BOTH, axis=0, tiled=False)
        top = jnp.max(stats[:, 0], axis=0)
        total = jnp.sum(stats[:, 1] * jnp.exp(stats[:, 0] - top[None]), axis=0)
        norm = jnp.stack([top, 1.0 / total])
        g_shard, d_top_part = head_grads(z_all, norm, tgts, embed_table, grad_embed, shard, n_wide, n_tiles, n_rep, True)
        d_top_part, act0, act1 = lax.optimization_barrier((d_top_part, act0, act1))
        d_top_own = lax.psum_scatter(d_top_part, BOTH, scatter_dimension=0, tiled=True)
        red_tile = rest0 + stage_id * n_red
        g_own = head_grads(z_all, norm, tgts, embed_table, grad_embed, blocks(red_tile, red_tile), n_red, n_red, n_rep, False)[0]
        d_top_own, g_own = lax.optimization_barrier((d_top_own, g_own))
        d_top_own = d_top_own.reshape(d_model, -1).T.astype(jnp.bfloat16)
        d_top = lax.all_gather(d_top_own, BOTH, axis=0, tiled=True)
        g_shard, d_top_own = lax.optimization_barrier((g_shard, d_top_own))
        g_far = other(g_own)
        g_wide = lax.all_gather(g_shard, BOTH, axis=0, tiled=True)

        d_half = lax.dynamic_slice_in_dim(d_top, stage_id * half, half)
        d_act1, g_in1, g_out1 = block_backward(d_half, act1, w_in1, w_out1)
        d_low_half, g_in0, g_out0 = block_backward(d_act1, act0, w_in0, w_out0)
        my_rank = lax.dynamic_slice_in_dim(rank, stage_id * half, half)
        perm = (my_rank[None, :] == order[:, None]).astype(jnp.bfloat16)
        low_half = jnp.dot(perm, d_low_half, preferred_element_type=jnp.float32).astype(jnp.bfloat16)
        low = low_half + other(low_half)

        def both_halves(part0, part1):
            far0, far1 = lax.ppermute(part0, 'stage', [(1, 0)]), lax.ppermute(part1, 'stage', [(0, 1)])
            return jnp.where(low_core, part0 + far0, part1 + far1)

        full_first = grad_first[0] + both_halves(g_in0, g_in1) / n_rep
        full_second = grad_second[0] + both_halves(g_out0, g_out1) / n_rep
        my_part = lax.axis_index('data') * n_part
        embed_sq = (jnp.sum(rows_sumsq(blocks(dev_id * n_wide, 0), starts, sorted_ids, low, g_shard, n_wide, low_scale))
                    + jnp.sum(rows_sumsq(blocks(red_tile + my_part, my_part), starts, sorted_ids, low, g_own, n_part, low_scale)))
        stage_sq = jnp.sum(full_first * full_first) + jnp.sum(full_second * full_second)
        parts_sq = lax.all_gather(jnp.full((1, 128), embed_sq + stage_sq / n_rep), BOTH, axis=0, tiled=True)
        total_sq = jnp.sum(parts_sq[:, 0])
        clip_scale = jnp.minimum(1.0, max_norm[0] / (jnp.sqrt(total_sq) + CLIP_EPS))
        new_first, new_mom_first, new_vel_first = adamw_update(w_first[0], mom_first[0], vel_first[0], full_first, clip_scale)
        new_second, new_mom_second, new_vel_second = adamw_update(w_second[0], mom_second[0], vel_second[0], full_second, clip_scale)
        new_embed, new_mom_embed, new_vel_embed = embed_adam(
            starts, blocks(stage_id), clip_scale.reshape(1), sorted_ids, low, g_wide, g_own, g_far, embed_table, mom_embed, vel_embed, low_scale)

        next_in, next_out = new_first.astype(jnp.bfloat16), new_second.astype(jnp.bfloat16)
        next_in0, next_in1 = by_stage(next_in, other(next_in))
        next_out0, next_out1 = by_stage(next_out, other(next_out))
        n_micro, tokens = next_tokens.shape
        my_micro = n_micro // n_stage
        my_rows = lax.dynamic_slice_in_dim(next_tokens, stage_id * my_micro, my_micro).reshape(2, -1)
        gathered = []
        for piece in range(2):
            final_act = next_forward(my_rows[piece], new_embed, next_in0, next_out0, next_in1, next_out1, scale_in)
            gathered.append(lax.all_gather(final_act.reshape(my_micro // 2, tokens, d_model), 'stage', axis=0, tiled=False))
        next_acts = jnp.stack(gathered, axis=1).reshape(n_micro, tokens, d_model)
        return (new_first[None], new_second[None], new_mom_first[None], new_mom_second[None],
                new_vel_first[None], new_vel_second[None], new_embed, new_mom_embed, new_vel_embed, next_acts)

    return jax.shard_map(local_step, mesh=mesh, in_specs=in_specs, out_specs=out_specs, check_vma=False)
```

time: 2190 us -> 887 us (0.41)
  waiting for transfers between devices: 1170 us -> 45.3 us
  Pallas kernels: 0 us -> 578 us
  other arithmetic: 495 us -> 128 us
  local copies, waits for them, and re-layouts: 350 us -> 25.5 us
  matrix products: 117 us -> 19 us
  blocking collectives: 3.15 us -> 46.2 us
    psum x3 -> x0, waiting for transfers between devices: 877 us -> none  [the longest x1 717 us: local_step(): lax.psum(head_grad + low_grad, ('data', 'stage')) / n_rep]
    pallas_call x0 -> x10, Pallas kernels: none -> 578 us  [the longest x1 178 us: embed_adam(): pl.pallas_call(functools.partial(adam_kernel, low_scale, n_wide, n_red),...]
    ppermute x3 -> x12, waiting for transfers between devices: 292 us -> 4.26 us  [the longest x1 2.5 us: local_step(): lax.ppermute(z_own[:cut], 'stage', [(1, 0)])]
    gather x1 -> x0, local copies, waits for them, and re-layouts: 266 us -> none  [local_step(): jnp.take(next_table, next_tokens.reshape(-1), axis=0).astype(jnp.float32)]
    convert_element_type x8 -> x5, other arithmetic: 251 us -> 27.2 us  [the longest x1 11.3 us: local_step(): new_second.astype(jnp.bfloat16)]
    scatter-add x1 -> x0, other arithmetic: 121 us -> none  [local_step(): jax.ops.segment_sum(d_low.astype(jnp.float32), last_tokens, num_segments=...]
    dot_general x1, matrix products: 90 us -> 7.92 us  [block_forward(): mlp_out = jnp.dot(hidden, w_out, preferred_element_type=jnp.float32)]
    add x1, other arithmetic: 63 us -> 6.66 us  [local_step(): low = low_half + other(low_half)]
  transfers between devices with their start and end apart: 6 -> 19, of which waited for: 5 -> 5; matrix products, arithmetic and copies ran while one was open for 10% -> 13% of each run, Pallas kernels for 0% -> 38%
where the time goes in v1:
time: 887 us; the launch traced here: 880 us
  Pallas kernels  578 us (65%)
  other arithmetic  128 us (14%)
  blocking collectives  46.2 us (5%)
  waiting for transfers between devices  45.3 us (5%)
  local copies, waits for them, and re-layouts  25.5 us (3%)
  starting transfers between devices  19.4 us (2%)
  matrix products  19 us (2%)
  between operations  19 us (2%)
    pallas_call x1, Pallas kernels, embed_adam(): pl.pallas_call(functools.partial(adam_kernel, low_scale, n_wide, n_red),...  178 us
    pallas_call x2, Pallas kernels, head_grads(): pl.pallas_call(functools.partial(head_kernel, vocab, n_chunks, n_rep, n_o...  144 us
    pallas_call x2, Pallas kernels, next_forward(): pl.pallas_call(functools.partial(next_kernel, scale, n_tok // TOKEN_BLOCK...  127 us
    pallas_call x2, Pallas kernels, block_backward(): pl.pallas_call(functools.partial(backward_kernel, n_chunks), out_shape=[j...  75.5 us
    pallas_call x1, Pallas kernels, head_stats(): pl.pallas_call(functools.partial(stats_kernel, vocab, n_tok // CHUNK, n_o...  35.1 us
    unnamed x1, blocking collectives  23.1 us
    all_gather x1, waiting for transfers between devices, local_step(): d_top = lax.all_gather(d_top_own, BOTH, axis=0, tiled=True)  20.3 us
    all_gather x2, waiting for transfers between devices, local_step(): lax.all_gather(final_act.reshape(my_micro // 2, tokens, d_model), 'stage'...  20.1 us
  transfers between devices with their start and end apart: 19, of which 5 were waited for; matrix products, arithmetic and copies ran while one was open for 13% of the time, Pallas kernels for 38%

profile of v1, /device:TPU:0, one launch (start us, length us, event | category | flops | bytes accessed | tf_op | source)
XLA Modules:
  0.0 879.8 jit_solution(12662089657152519173)
XLA Ops:
  7.2 2.5 bitcast_convert_fusion
  9.8 7.9 add_convert_fusion
  18.8 1.3 collective-permute-start
  20.1 2.5 collective-permute-done
  22.6 1.9 slice_select_fusion
  24.6 10.0 %all_gather.31 = s32[2,4096]{1,0:T(2,128)S(1)} all-gather(s32[2,1024]{1,0:T(2,128)S(1)} %pad_add_fusion), channel_id=1, replica_groups=mesh['data'=4,'stage'=2] {'data'}, dimensions={1}, use_global_device_ids=true | all-gather | bytes 40960 | tf_op jit(solution)/shard_map/all_gather | solution.py:433
  36.1 19.7 %convert_reduce_fusion = s32[4096]{0:T(1024)S(1)} fusion(s32[4096]{0:T(1024)S(1)} %bitcast.145), kind=kLoop, calls=%fused_computation.2 | loop fusion | flops 117436416 | bytes 32768 | tf_op jit(solution)/shard_map/reduce_sum | solution.py:441
  55.8 10.6 %select_reduce_fusion = s32[4096]{0:T(1024)} fusion(s32[4096]{0:T(1024)S(1)} %convert_reduce_fusion, s32[4096]{0:T(1024)S(1)} %bitcast.146), kind=kLoop, calls=%fused_computation | loop fusion | flops 50327552 | bytes 49152 | tf_op jit(solution)/shard_map/reduce_sum | solution.py:442
  67.1 35.1 %head_stats.1 = f32[2,4096]{1,0:T(2,128)} custom-call(s32[2]{0:T(128)} %pad_add_fusion.2.blk_ref, bf16[4096,512]{1,0:T(8,128)(2,1)} %all-gather.9.cloned.1.call-done.z_ref, f32[32128,512]{1,0:T(8,128)} %w_ref.1), custom_call_target="tpu_custom_call" | custom-call | flops 17179869184 | bytes 8388608 | tf_op jit(solution)/shard_map/head_stats/pallas_call | solution.py:154
  102.2 13.0 %all-gather.1 = f32[8,2,4096]{2,1,0:T(2,128)S(1)} all-gather(f32[1,2,4096]{2,1,0:T(2,128)} %bitcast.143), channel_id=3, replica_groups=mesh['data'=4,'stage'=2] {'data','stage'}, dimensions={0}, use_global_device_ids=true | all-gather | bytes 294912 | tf_op jit(solution)/shard_map/all_gather | solution.py:457
  116.3 3.0 constant_dynamic-slice_fusion.1
  119.3 70.5 %head_grads.1 = (f32[2560,512]{1,0:T(8,128)}, f32[8,512,512]{2,1,0:T(8,128)}) custom-call(s32[2]{0:T(128)} %pad_add_fusion.2.blk_ref, bf16[4096,512]{1,0:T(8,128)(2,1)} %all-gather.9.cloned.1.call-done.z_ref, f32[2,4096]{1,0:T(2,128)} %pad_maximum_fusion.1.norm_ref, s32[1,4096]{1,0:T(1,128)} %get-tuple-element.81.tgt_ref, f32[32128,512]{1,0:T(8,128)} %w_ref.1, ...), custom_call_target="tpu_custom_call" | custom-call | flops 51539607552 | bytes 25165824 | tf_op jit(solution)/shard_map/head_grads/pallas_call | solution.py:214
  189.9 5.0 broadcast_select_fusion.8
  194.9 9.1 %copy.35 = f32[8,512,512]{1,2,0:T(8,128)} copy(f32[8,512,512]{2,1,0:T(8,128)} %get-tuple-element.38) | data formatting | bytes 16777216 | tf_op jit(solution)/shard_map/optimization_barrier | solution.py:462
  204.7 73.4 %head_rows.1.g_ref.go_ref = f32[6144,512]{1,0:T(8,128)} custom-call(s32[2]{0:T(128)} %pad_add_fusion.3.blk_ref, bf16[4096,512]{1,0:T(8,128)(2,1)} %all-gather.9.cloned.1.call-done.z_ref, f32[2,4096]{1,0:T(2,128)} %pad_maximum_fusion.1.norm_ref, s32[1,4096]{1,0:T(1,128)} %get-tuple-element.81.tgt_ref, f32[32128,512]{1,0:T(8,128)} %w_ref.1, f32[32128,512]{1,0:T(8,128)} %g_ref.3), custom_call_target="tpu_custom_call" | custom-call | flops 51539607552 | bytes 37748736 | tf_op jit(solution)/shard_map/head_rows/pallas_call | solution.py:214
  278.1 2.1 convert_bitcast_fusion
  281.6 2.8 bitcast_convert_fusion.1
  285.4 2.4 broadcast_select_fusion.6
  288.5 2.4 broadcast_select_fusion.2
  290.9 20.3 %all-gather.13.cloned.1.call-done = bf16[4096,512]{1,0:T(8,128)(2,1)} async-done(((bf16[512,512]{1,0:T(8,128)(2,1)}), bf16[4096,512]{1,0:T(8,128)(2,1)}) %all-gather.13.cloned.1.call-update) | async-done | bytes 4194320 | tf_op jit(solution)/shard_map/all_gather | solution.py:468
  311.2 3.0 constant_dynamic-slice_fusion.g_ref
  314.2 37.8 %block_backward.2 = (bf16[2048,512]{1,0:T(8,128)(2,1)}, f32[512,2048]{1,0:T(8,128)}, f32[2048,512]{1,0:T(8,128)}) custom-call(bf16[2048,512]{1,0:T(8,128)(2,1)} %constant_dynamic-slice_fusion.g_ref, bf16[2048,512]{1,0:T(8,128)(2,1)} %get-tuple-element.40.x_ref, bf16[512,2048]{1,0:T(8,128)(2,1)} %get-tuple-element.75.wi_ref, ...), custom_call_target="tpu_custom_call" | custom-call | flops 21474836480 | bytes 12582912 | tf_op jit(solution)/shard_map/block_backward/pallas_call | solution.py:85
  352.0 37.8 %block_backward.3 = (bf16[2048,512]{1,0:T(8,128)(2,1)}, f32[512,2048]{1,0:T(8,128)}, f32[2048,512]{1,0:T(8,128)}) custom-call(bf16[2048,512]{1,0:T(8,128)(2,1)} %get-tuple-element.41.g_ref, bf16[2048,512]{1,0:T(8,128)(2,1)} %get-tuple-element.42.x_ref, bf16[512,2048]{1,0:T(8,128)(2,1)} %get-tuple-element.74.wi_ref, bf16[2048,512]{1,0:T(8,128)(2,1)} %get-tuple-element.72.wo_ref), custom_call_target="tpu_custom_call" | custom-call | flops 21474836480 | bytes 12582912 | tf_op jit(solution)/shard_map/block_backward/pallas_call | solution.py:85
  389.8 11.1 %fusion.12 = bf16[4096,512]{1,0:T(8,128)(2,1)S(1)} fusion(bf16[2048,512]{1,0:T(8,128)(2,1)} %get-tuple-element.43, s32[2048]{0:T(1024)S(1)} %dynamic-slice-done), kind=kOutput, calls=%fused_computation.21 | convolution fusion | flops 8600420352 | bytes 6299648 | tf_op jit(solution)/shard_map/dot_general | solution.py:478
  400.9 2.0 copy-done.7
  403.4 1.3 collective-permute-start.7
  404.7 7.0 collective-permute-start.8
  411.7 1.3 collective-permute-start.5
  413.0 2.0 copy-done.8
  415.0 6.9 collective-permute-start.6
  422.6 6.7 add.109.low_ref
  429.3 7.8 rows_sumsq.3
  437.1 10.0 %rows_sumsq.2 = f32[8,512]{1,0:T(8,128)} custom-call(s32[2]{0:T(128)} %get-tuple-element.83.blk_ref, s32[65]{0:T(128)} %convert_reduce_fusion.1.start_ref, s32[32,128]{1,0:T(8,128)} %bitcast.141, bf16[4096,512]{1,0:T(8,128)(2,1)} %add.109.low_ref, f32[2560,512]{1,0:T(8,128)} %get-tuple-element.45.g_ref), custom_call_target="tpu_custom_call" | custom-call | tf_op jit(solution)/shard_map/rows_sumsq/pallas_call | solution.py:259
  447.7 1.3 reduce_sum.85
  449.0 12.8 %multiply_reduce_fusion = (f32[]{:T(128)}, f32[2048,512]{1,0:T(8,128)}) fusion(f32[2048,512]{1,0:T(8,128)} %get-tuple-element.50, f32[2048,512]{1,0:T(8,128)} %collective-permute-done.8, f32[2048,512]{1,0:T(8,128)} %get-tuple-element.49, f32[2048,512]{1,0:T(8,128)} %collective-permute-done.7, pred[]{:T(512)S(6)} %eq.14, f32[1,2048,512]{2,1,0:T(8,128)} %param.24), kind=kLoop, calls=%fused_computation.38 | loop fusion | flops 7340031 | bytes 25165828 | tf_op jit(solution)/shard_map/reduce_sum | solution.py:490
  461.8 10.9 %multiply_reduce_fusion.1 = (f32[]{:T(128)}, f32[512,2048]{1,0:T(8,128)}) fusion(f32[512,2048]{1,0:T(8,128)} %get-tuple-element.48, f32[512,2048]{1,0:T(8,128)} %collective-permute-done.6, f32[512,2048]{1,0:T(8,128)} %get-tuple-element.47, f32[512,2048]{1,0:T(8,128)} %collective-permute-done.5, pred[]{:T(512)S(6)} %eq.14, f32[1,512,2048]{2,1,0:T(8,128)S(1)} %copy-done.4), kind=kLoop, calls=%fused_computation.39 | loop fusion | flops 7340031 | bytes 25165828 | tf_op jit(solution)/shard_map/reduce_sum | solution.py:490
  476.1 23.1 %all-reduce = f32[8]{0:T(128)S(1)} all-reduce(f32[8]{0:T(128)S(1)} %dynamic-update-slice), channel_id=2, replica_groups=mesh['data'=4,'stage'=2] {'data','stage'}, use_global_device_ids=true, to_apply=%add | all-reduce | flops 8 | bytes 64
  500.7 11.3 %fusion.45 = (bf16[2048,512]{1,0:T(8,128)(2,1)S(1)}, f32[2048,512]{1,0:T(8,128)}, f32[1,2048,512]{2,1,0:T(8,128)}, f32[1,2048,512]{2,1,0:T(8,128)}) fusion(f32[1,2048,512]{2,1,0:T(8,128)} %param.22, f32[2048,512]{1,0:T(8,128)} %get-tuple-element.59, f32[]{:T(128)} %min.3, f32[1,2048,512]{2,1,0:T(8,128)} %param.20, f32[1,2048,512]{2,1,0:T(8,128)} %param.18), kind=kLoop, calls=%fused_computation.87 | loop fusion | flops 17825792 | bytes 31457284 | tf_op jit(solution)/shard_map/convert_element_type | solution.py:499
  512.0 1.4 copy-done.3
  514.5 1.2 copy-done.6
  515.7 8.5 fusion.46
  524.9 3.8 broadcast_select_fusion.4
  528.8 4.5 broadcast_select_fusion
  533.2 177.9 %embed_adam.1 = (f32[32128,512]{1,0:T(8,128)}, f32[32128,512]{1,0:T(8,128)}, f32[32128,512]{1,0:T(8,128)}) custom-call(s32[65]{0:T(128)} %convert_reduce_fusion.1.start_ref, s32[1]{0:T(128)} %bitcast.34.stage_ref, f32[1]{0:T(128)} %bitcast.35.clip_ref, s32[32,128]{1,0:T(8,128)} %bitcast.142, bf16[4096,512]{1,0:T(8,128)(2,1)} %add.109.low_ref, ...), custom_call_target="tpu_custom_call" | custom-call | flops 328990720 | bytes 460587008 | tf_op jit(solution)/shard_map/embed_adam/pallas_call | solution.py:321
  711.1 63.6 %next_forward.2 = bf16[4096,512]{1,0:T(8,128)(2,1)} custom-call(s32[4096]{0:T(1024)} %get-tuple-element.86.ids_ref, f32[32128,512]{1,0:T(8,128)} %get-tuple-element.28.table_ref, bf16[512,2048]{1,0:T(8,128)(2,1)} %get-tuple-element.71.wi0_ref, bf16[2048,512]{1,0:T(8,128)(2,1)} %get-tuple-element.69.wo0_ref, bf16[512,2048]{1,0:T(8,128)(2,1)} %get-tuple-element.70.wi1_ref, ...), custom_call_target="tpu_custom_call" | custom-call | flops 34359738368 | bytes 12582912 | tf_op jit(solution)/shard_map/next_forward/pallas_call | solution.py:381
  774.8 63.7 %next_forward.3 = bf16[4096,512]{1,0:T(8,128)(2,1)} custom-call(s32[4096]{0:T(1024)} %get-tuple-element.85.ids_ref, f32[32128,512]{1,0:T(8,128)} %get-tuple-element.28.table_ref, bf16[512,2048]{1,0:T(8,128)(2,1)} %get-tuple-element.71.wi0_ref, bf16[2048,512]{1,0:T(8,128)(2,1)} %get-tuple-element.69.wo0_ref, bf16[512,2048]{1,0:T(8,128)(2,1)} %get-tuple-element.70.wi1_ref, ...), custom_call_target="tpu_custom_call" | custom-call | flops 34359738368 | bytes 12582912 | tf_op jit(solution)/shard_map/next_forward/pallas_call | solution.py:381
  838.6 20.1 %all-gather.19.cloned.1.call-done = bf16[2,4,1024,512]{3,2,1,0:T(8,128)(2,1)} async-done(((bf16[1,4,1024,512]{3,2,1,0:T(8,128)(2,1)}), bf16[2,4,1024,512]{3,2,1,0:T(8,128)(2,1)}) %all-gather.19.cloned.1.call-update) | async-done | bytes 8388624 | tf_op jit(solution)/shard_map/all_gather | solution.py:508
  858.7 13.8 %pad_maximum_fusion = bf16[2,2,4,1024,512]{4,3,2,1,0:T(8,128)(2,1)} fusion(bf16[2,1,4,1024,512]{4,3,2,1,0:T(8,128)(2,1)} %bitcast.133, bf16[2,1,4,1024,512]{4,3,2,1,0:T(8,128)(2,1)} %bitcast.132), kind=kLoop, calls=%fused_computation.8 | loop fusion | flops 8388608 | bytes 33554432 | tf_op jit(solution)/shard_map/stack | solution.py:509
  (83 shorter events, 12.7 us)
Async XLA Ops:
  7.2 2.6 copy-start.9
  7.2 59.2 %all-gather.9.cloned.1.call-start = ((), (), s32[]{:S(2)}) async-start(), calls=%async_computation.1 | async-start | bytes 4718592 | tf_op jit(solution)/shard_map/all_gather | solution.py:437
  9.8 14.8 %copy-start.13 = (s32[1024]{0:T(1024)S(1)}, s32[1024]{0:T(1024)}, u32[]{:S(2)}) copy-start(s32[1024]{0:T(1024)} %param.31) | copy-start | bytes 12292
  9.8 14.8 %copy-start.14 = (s32[1024]{0:T(1024)S(1)}, s32[1024]{0:T(1024)}, u32[]{:S(2)}) copy-start(s32[1024]{0:T(1024)} %param.30) | copy-start | bytes 12292
  18.8 3.8 collective-permute-start
  24.5 91.7 %all-gather.11.cloned.1.call-start = ((), (), s32[]{:S(2)}) async-start(), calls=%async_computation.2 | async-start | bytes 5242880 | tf_op jit(solution)/shard_map/all_gather | solution.py:447
  55.8 235.2 %copy-start.12 = (s32[4096]{0:T(1024)}, s32[4096]{0:T(1024)S(1)}, u32[]{:S(2)}) copy-start(s32[4096]{0:T(1024)S(1)} %convert_reduce_fusion) | copy-start | bytes 49156
  66.4 211.6 %reduce-scatter.2.cloned.1.call-start = ((), (), s32[]{:S(2)}) async-start(), calls=%async_computation.3 | async-start | bytes 9437184 | tf_op jit(solution)/shard_map/reduce_scatter | solution.py:463
  119.3 70.5 %collective-permute-start.1 = (bf16[2048,512]{1,0:T(8,128)(2,1)}, bf16[2048,512]{1,0:T(8,128)(2,1)}, u32[]{:S(2)}, u32[]{:S(2)}) collective-permute-start(bf16[2048,512]{1,0:T(8,128)(2,1)} %constant_dynamic-slice_fusion.1), channel_id=1, source_target_pairs={{0,1},{1,0},{2,3},{3,2},{4,5},{5,4},{6,7},{7,6}} | collective-permute-start | bytes 6291464 | tf_op jit(solution)/shard_map/ppermute | solution.py:421
  204.0 107.1 %all-gather.13.cloned.1.call-start = ((), (), s32[]{:S(2)}) async-start(), calls=%async_computation.4 | async-start | bytes 4718592 | tf_op jit(solution)/shard_map/all_gather | solution.py:468
  280.2 253.1 %all-gather.15.cloned.1.call-start = ((), (), s32[]{:S(2)}) async-start(), calls=%async_computation.5 | async-start | bytes 47185920 | tf_op jit(solution)/shard_map/all_gather | solution.py:471
  280.8 557.8 %all-gather.17.cloned.1.call-start = ((), (), s32[]{:S(2)}) async-start(), calls=%async_computation.6 | async-start | bytes 12582912 | tf_op jit(solution)/shard_map/all_gather | solution.py:508
  281.1 4.3 copy-start
  281.1 4.3 collective-permute-start.3
  284.3 4.2 copy-start.1
  284.4 4.2 collective-permute-start.2
  352.0 37.8 %dynamic-slice-start = ((s32[4096]{0:T(1024)}, s32[]{:T(128)}), s32[2048]{0:T(1024)S(1)}, s32[]{:S(2)}) async-start(s32[4096]{0:T(1024)} %copy-done.12, s32[]{:T(128)} %select_n.86), calls=%async_computation.8 | async-start | bytes 16896 | tf_op jit(solution)/shard_map/dynamic_slice | solution.py:476
  400.9 2.0 copy-start.7
  402.9 10.1 %collective-permute-start.4 = (bf16[4096,512]{1,0:T(8,128)(2,1)S(1)}, bf16[4096,512]{1,0:T(8,128)(2,1)S(1)}, u32[]{:S(2)}, u32[]{:S(2)}) collective-permute-start(bf16[4096,512]{1,0:T(8,128)(2,1)S(1)} %fusion.12), channel_id=1, source_target_pairs={{0,1},{1,0},{2,3},{3,2},{4,5},{5,4},{6,7},{7,6}} | collective-permute-start | bytes 12582920 | tf_op jit(solution)/shard_map/ppermute | solution.py:421
  403.2 130.1 %collective-permute-start.9 = (f32[6144,512]{1,0:T(8,128)}, f32[6144,512]{1,0:T(8,128)}, u32[]{:S(2)}, u32[]{:S(2)}) collective-permute-start(f32[6144,512]{1,0:T(8,128)} %head_rows.1.g_ref.go_ref), channel_id=1, source_target_pairs={{0,1},{1,0},{2,3},{3,2},{4,5},{5,4},{6,7},{7,6}} | collective-permute-start | bytes 37748744 | tf_op jit(solution)/shard_map/ppermute | solution.py:421
  403.4 45.6 %collective-permute-start.7 = (f32[2048,512]{1,0:T(8,128)}, f32[2048,512]{1,0:T(8,128)}, u32[]{:S(2)}, u32[]{:S(2)}) collective-permute-start(f32[2048,512]{1,0:T(8,128)} %get-tuple-element.49), channel_id=1, source_target_pairs={{1,0},{3,2},{5,4},{7,6}} | collective-permute-start | bytes 12582920 | tf_op jit(solution)/shard_map/ppermute | solution.py:482
  404.7 44.3 %collective-permute-start.8 = (f32[2048,512]{1,0:T(8,128)}, f32[2048,512]{1,0:T(8,128)}, u32[]{:S(2)}, u32[]{:S(2)}) collective-permute-start(f32[2048,512]{1,0:T(8,128)} %get-tuple-element.50), channel_id=1, source_target_pairs={{0,1},{2,3},{4,5},{6,7}} | collective-permute-start | bytes 12582920 | tf_op jit(solution)/shard_map/ppermute | solution.py:482
  411.7 50.1 %collective-permute-start.5 = (f32[512,2048]{1,0:T(8,128)}, f32[512,2048]{1,0:T(8,128)}, u32[]{:S(2)}, u32[]{:S(2)}) collective-permute-start(f32[512,2048]{1,0:T(8,128)} %get-tuple-element.47), channel_id=1, source_target_pairs={{1,0},{3,2},{5,4},{7,6}} | collective-permute-start | bytes 12582920 | tf_op jit(solution)/shard_map/ppermute | solution.py:482
  413.0 2.0 copy-start.8
  415.0 46.8 %collective-permute-start.6 = (f32[512,2048]{1,0:T(8,128)}, f32[512,2048]{1,0:T(8,128)}, u32[]{:S(2)}, u32[]{:S(2)}) collective-permute-start(f32[512,2048]{1,0:T(8,128)} %get-tuple-element.48), channel_id=1, source_target_pairs={{0,1},{2,3},{4,5},{6,7}} | collective-permute-start | bytes 12582920 | tf_op jit(solution)/shard_map/ppermute | solution.py:482
  437.1 10.0 %copy-start.10 = (f32[8,512]{1,0:T(8,128)S(1)}, f32[8,512]{1,0:T(8,128)}, u32[]{:S(2)}) copy-start(f32[8,512]{1,0:T(8,128)} %rows_sumsq.3) | copy-start | bytes 49156
  449.0 12.8 %copy-start.4 = (f32[1,512,2048]{2,1,0:T(8,128)S(1)}, f32[1,512,2048]{2,1,0:T(8,128)}, u32[]{:S(2)}) copy-start(f32[1,512,2048]{2,1,0:T(8,128)} %param.23) | copy-start | bytes 12582916
  500.6 11.3 %copy-start.2 = (f32[1,512,2048]{2,1,0:T(8,128)S(1)}, f32[1,512,2048]{2,1,0:T(8,128)}, u32[]{:S(2)}) copy-start(f32[1,512,2048]{2,1,0:T(8,128)} %param.17) | copy-start | bytes 12582916
  500.6 12.7 %copy-start.3 = (f32[512,2048]{1,0:T(8,128)S(1)}, f32[512,2048]{1,0:T(8,128)}, u32[]{:S(2)}) copy-start(f32[512,2048]{1,0:T(8,128)} %get-tuple-element.61) | copy-start | bytes 12582916
  500.6 13.9 %copy-start.5 = (f32[1,512,2048]{2,1,0:T(8,128)S(1)}, f32[1,512,2048]{2,1,0:T(8,128)}, u32[]{:S(2)}) copy-start(f32[1,512,2048]{2,1,0:T(8,128)} %param.21) | copy-start | bytes 12582916
  500.6 15.1 %copy-start.6 = (f32[1,512,2048]{2,1,0:T(8,128)S(1)}, f32[1,512,2048]{2,1,0:T(8,128)}, u32[]{:S(2)}) copy-start(f32[1,512,2048]{2,1,0:T(8,128)} %param.19) | copy-start | bytes 12582916
  511.9 13.0 %collective-permute-start.11 = (bf16[2048,512]{1,0:T(8,128)(2,1)S(1)}, bf16[2048,512]{1,0:T(8,128)(2,1)}, u32[]{:S(2)}, u32[]{:S(2)}) collective-permute-start(bf16[2048,512]{1,0:T(8,128)(2,1)S(1)} %get-tuple-element.54), channel_id=1, source_target_pairs={{0,1},{1,0},{2,3},{3,2},{4,5},{5,4},{6,7},{7,6}} | collective-permute-start | bytes 6291464 | tf_op jit(solution)/shard_map/ppermute | solution.py:421
  515.7 8.5 copy-start.11
  524.3 4.5 collective-permute-start.10
  774.8 83.9 %all-gather.19.cloned.1.call-start = ((), (), s32[]{:S(2)}) async-start(), calls=%async_computation.7 | async-start | bytes 12582912 | tf_op jit(solution)/shard_map/all_gather | solution.py:508
Sparse Core Ops, SparseCore 0:
  24.6 33.5 all-gather.8
  66.5 48.0 all-gather.10
  204.2 62.3 reduce-scatter.1
  280.3 30.8 all-gather.12
  313.4 192.9 all-gather.14
  774.9 19.9 all-gather.16
  838.7 19.9 all-gather.18

commit v2 on v1

--- a/solution.py
+++ b/solution.py
@@ -18,9 +18,12 @@
 TILE = 512
 ADAM_TILE = 1024
 CHUNK = 512
-SEG = 128
+SEG = 256
 TOKEN_BLOCK = 512
 FF_CHUNK = 512
+FWD_CHUNK = 1024
+N_DEV = 8
+MESH_ID = pl.DeviceIdType.MESH
 WIDE_TILES = 5
 NEG = -1e30
 GELU_K = math.sqrt(2.0 / math.pi)
@@ -166,7 +169,7 @@
 
 
 def head_kernel(vocab, n_chunks, n_rep, n_own, with_top, blk_ref, z_ref, norm_ref, tgt_ref, e_ref, g_ref, out_ref, *rest):
-    top_ref = rest[0] if with_top else None
+    top_ref = rest[1] if with_top else None
     acc_ref = rest[-1]
     j = pl.program_id(0)
     rows, valid, e_tile, bias = load_rows(tile_of(n_own, blk_ref, j), e_ref, vocab)
@@ -200,6 +203,13 @@
         def _():
             lax.fori_loop(0, n_chunks, functools.partial(chunk, False), 0, unroll=2)
 
+        @pl.when(j == pl.num_programs(0) - 1)
+        def _():
+            def turn(c, _):
+                rest[0][c] = top_ref[c].T
+                return 0
+            lax.fori_loop(0, n_chunks, turn, 0)
+
 
 def head_grads(z_all, norm, targets, embed_table, grad_embed, blocks, n_own, n_tiles, n_rep, with_top):
     vocab, d_model = embed_table.shape
@@ -209,8 +219,8 @@
     out_shape = [jax.ShapeDtypeStruct((n_own * TILE, d_model), jnp.float32)]
     out_specs = [pl.BlockSpec((TILE, d_model), lambda j, b: (jnp.minimum(j, n_own - 1), 0))]
     if with_top:
-        out_shape.append(jax.ShapeDtypeStruct((n_chunks, d_model, CHUNK), jnp.float32))
-        out_specs.append(pl.BlockSpec((n_chunks, d_model, CHUNK), lambda j, b: (0, 0, 0)))
+        out_shape.append(jax.ShapeDtypeStruct((n_chunks, CHUNK, d_model), jnp.float32))
+        out_specs.append(pl.BlockSpec((n_chunks, CHUNK, d_model), lambda j, b: (0, 0, 0), pipeline_mode=pl.Buffered(1)))
     return pl.pallas_call(
         functools.partial(head_kernel, vocab, n_chunks, n_rep, n_own, with_top),
         out_shape=out_shape,
@@ -222,7 +232,7 @@
                       pl.BlockSpec((TILE, d_model), lambda j, b: (jnp.minimum(tile_of(n_own, b, j), last), 0)),
                       pl.BlockSpec((TILE, d_model), lambda j, b: (jnp.minimum(b[0] + jnp.minimum(j, n_own - 1), last), 0))],
             out_specs=out_specs,
-            scratch_shapes=[pltpu.VMEM((TILE, d_model), jnp.float32)]),
+            scratch_shapes=[pltpu.VMEM((n_chunks, d_model, CHUNK), jnp.float32)] * with_top + [pltpu.VMEM((TILE, d_model), jnp.float32)]),
         compiler_params=params(),
         cost_estimate=pl.CostEstimate(flops=(6 if with_top else 4) * n_tiles * TILE * n_tok * d_model,
                                       bytes_accessed=n_tiles * TILE * d_model * 12, transcendentals=0),
@@ -276,27 +286,31 @@
     own = n_wide + n_red * stage_ref[0]
     is_own = (j >= own) & (j < own + n_red)
 
+    rows = j * ADAM_TILE + lax.broadcasted_iota(jnp.int32, (ADAM_TILE, 1), 0)
+    per = ADAM_TILE // TILE
+    first = jnp.minimum(start_ref[per * j] // SEG, ids_ref.shape[0] - 1)
+
+    def segment(c):
+        pick = jnp.where(rows == ids_ref[pl.ds(c, 1), :], 1.0, 0.0).astype(jnp.bfloat16)
+        return low_scale * jnp.dot(pick, low_ref[pl.ds(pl.multiple_of(c * SEG, SEG), SEG), :], preferred_element_type=jnp.float32)
+
     @pl.when(j < n_wide)
     def _():
-        acc_ref[...] = gw_ref[...]
+        acc_ref[...] = gw_ref[...] + segment(first)
 
     @pl.when(is_own)
     def _():
-        acc_ref[...] = go_ref[...]
+        acc_ref[...] = go_ref[...] + segment(first)
 
     @pl.when((j >= n_wide) & jnp.logical_not(is_own))
     def _():
-        acc_ref[...] = gf_ref[...]
-
-    rows = j * ADAM_TILE + lax.broadcasted_iota(jnp.int32, (ADAM_TILE, 1), 0)
-
-    def segment(c, _):
-        pick = jnp.where(rows == ids_ref[pl.ds(c, 1), :], 1.0, 0.0).astype(jnp.bfloat16)
-        acc_ref[...] += low_scale * jnp.dot(pick, low_ref[pl.ds(pl.multiple_of(c * SEG, SEG), SEG), :], preferred_element_type=jnp.float32)
+        acc_ref[...] = gf_ref[...] + segment(first)
+
+    def add(c, _):
+        acc_ref[...] += segment(c)
         return 0
 
-    per = ADAM_TILE // TILE
-    lax.fori_loop(start_ref[per * j] // SEG, (start_ref[per * j + per] + SEG - 1) // SEG, segment, 0)
+    lax.fori_loop(first + 1, (start_ref[per * j + per] + SEG - 1) // SEG, add, 0)
 
     def part(i, _):
         r = pl.ds(pl.multiple_of(i * 32, 32), 32)
@@ -338,7 +352,7 @@
 def next_kernel(scale, n_blocks, ids_ref, table_ref, wi0_ref, wo0_ref, wi1_ref, wo1_ref, out_ref, rows_ref, x_ref, acc_ref, sems):
     blk = pl.program_id(0)
     slot = lax.rem(blk, 2)
-    n_ff = wi0_ref.shape[1] // FF_CHUNK
+    n_ff = wi0_ref.shape[1] // FWD_CHUNK
     per = TOKEN_BLOCK // (2 * n_ff)
 
     def fetch(base, to_slot, first, count):
@@ -355,23 +369,25 @@
 
     pltpu.make_async_copy(rows_ref.at[1 - slot], rows_ref.at[slot], sems.at[slot]).wait()
     base = jnp.minimum(blk + 1, n_blocks - 1) * TOKEN_BLOCK
-    more = blk + 1 < n_blocks
     x_ref[...] = (scale * rows_ref[slot].astype(jnp.bfloat16).astype(jnp.float32)).astype(jnp.bfloat16)
 
     for layer, (wi_ref, wo_ref) in enumerate(((wi0_ref, wo0_ref), (wi1_ref, wo1_ref))):
         acc_ref[...] = x_ref[...].astype(jnp.float32)
         for c in range(n_ff):
-            @pl.when(more)
-            def _():
-                fetch(base, 1 - slot, (layer * n_ff + c) * per, per)
-            cols = pl.ds(c * FF_CHUNK, FF_CHUNK)
+            fetch(base, 1 - slot, (layer * n_ff + c) * per, per)
+            cols = pl.ds(c * FWD_CHUNK, FWD_CHUNK)
             pre_act = jnp.dot(x_ref[...], wi_ref[:, cols], preferred_element_type=jnp.float32)
-            hidden = jax.nn.gelu(pre_act).astype(jnp.bfloat16)
+            bend = jnp.tanh(pre_act * (GELU_K + (GELU_K * GELU_A) * (pre_act * pre_act)))
+            hidden = ((0.5 * pre_act) * (1.0 + bend)).astype(jnp.bfloat16)
             acc_ref[...] += jnp.dot(hidden, wo_ref[cols, :], preferred_element_type=jnp.float32)
         if layer == 0:
             x_ref[...] = acc_ref[...].astype(jnp.bfloat16)
         else:
             out_ref[...] = acc_ref[...].astype(jnp.bfloat16)
+
+    @pl.when(blk == n_blocks - 1)
+    def _():
+        pltpu.make_async_copy(rows_ref.at[slot], rows_ref.at[1 - slot], sems.at[1 - slot]).wait()
 
 
 def next_forward(ids, table, wi0, wo0, wi1, wo1, scale):
@@ -391,6 +407,61 @@
         cost_estimate=pl.CostEstimate(flops=8 * n_tok * d_model * wi0.shape[1], bytes_accessed=6 * n_tok * d_model, transcendentals=0),
         name='next_forward',
     )(ids, table, wi0, wo0, wi1, wo1)
+
+
+def exchange(x_ref, all_ref, send_sems, recv_sems):
+    n_stage = lax.axis_size('stage')
+    me = lax.axis_index('data') * n_stage + lax.axis_index('stage')
+
+    def place(k):
+        to = lax.rem(me + k, N_DEV)
+        return to // n_stage, lax.rem(to, n_stage)
+
+    barrier = pltpu.get_barrier_semaphore()
+    for k in range(1, N_DEV):
+        pl.semaphore_signal(barrier, inc=1, device_id=place(k), device_id_type=MESH_ID)
+    pl.semaphore_wait(barrier, N_DEV - 1)
+    copies = []
+    for k in range(1, N_DEV):
+        copies.append(pltpu.make_async_remote_copy(
+            src_ref=x_ref, dst_ref=all_ref.at[k - 1], send_sem=send_sems.at[k - 1], recv_sem=recv_sems.at[k - 1],
+            device_id=place(k), device_id_type=MESH_ID))
+        copies[-1].start()
+    for copy in copies:
+        copy.wait()
+
+
+def norm_kernel(x_ref, out_ref, all_ref, send_sems, recv_sems):
+    exchange(x_ref, all_ref, send_sems, recv_sems)
+    top = x_ref[0:1, :]
+    for k in range(N_DEV - 1):
+        top = jnp.maximum(top, all_ref[k, 0:1, :])
+    total = x_ref[1:2, :] * jnp.exp(x_ref[0:1, :] - top)
+    for k in range(N_DEV - 1):
+        total += all_ref[k, 1:2, :] * jnp.exp(all_ref[k, 0:1, :] - top)
+    out_ref[0:1, :] = top
+    out_ref[1:2, :] = 1.0 / total
+
+
+def gather_kernel(x_ref, out_ref, all_ref, send_sems, recv_sems):
+    exchange(x_ref, all_ref, send_sems, recv_sems)
+    me = lax.axis_index('data') * lax.axis_size('stage') + lax.axis_index('stage')
+    out_ref[pl.ds(me, 1)] = x_ref[...][None]
+    for k in range(N_DEV - 1):
+        out_ref[pl.ds(lax.rem(me + (N_DEV - 1 - k), N_DEV), 1)] = all_ref[k:k + 1]
+
+
+def small_exchange(body, x, out_shape, collective_id, name):
+    return pl.pallas_call(
+        body,
+        out_shape=out_shape,
+        in_specs=[pl.BlockSpec(memory_space=pltpu.VMEM)],
+        out_specs=pl.BlockSpec(memory_space=pltpu.VMEM),
+        scratch_shapes=[pltpu.VMEM((N_DEV - 1,) + x.shape, x.dtype), pltpu.SemaphoreType.DMA((N_DEV - 1,)),
+                        pltpu.SemaphoreType.DMA((N_DEV - 1,))],
+        compiler_params=pltpu.CompilerParams(collective_id=collective_id, has_side_effects=True),
+        name=name,
+    )(x)
 
 
 def solution(mesh):
@@ -439,34 +510,32 @@
         order = jnp.arange(n_tok, dtype=jnp.int32)
         before = (ids[None, :] < ids[:, None]) | ((ids[None, :] == ids[:, None]) & (order[None, :] < order[:, None]))
         rank = jnp.sum(before.astype(jnp.int32), axis=1)
-        sorted_ids = jnp.sum(jnp.where(rank[None, :] == order[:, None], ids[None, :], 0), axis=1).reshape(n_tok // SEG, SEG)
         edges = TILE * jnp.arange(n_tiles * n_dev + 1, dtype=jnp.int32)
         starts = jnp.sum((ids[None, :] < edges[:, None]).astype(jnp.int32), axis=1)
-        z_all, rank, sorted_ids, starts, acts_in = lax.optimization_barrier((z_all, rank, sorted_ids, starts, stage_acts[0]))
+        z_all, rank, starts, acts_in = lax.optimization_barrier((z_all, rank, starts, stage_acts[0]))
 
         acts = lax.all_gather(acts_in, 'data', axis=0, tiled=True)
+
+        def blocks(*tiles):
+            return jnp.stack([jnp.asarray(t, jnp.int32) for t in tiles])
+
+        shard = blocks(dev_id * n_wide, rest0 + dev_id * n_rest - n_wide)
+        stat = head_stats(z_all, embed_table, shard, n_wide, n_tiles)
+        norm = small_exchange(norm_kernel, stat, jax.ShapeDtypeStruct(stat.shape, jnp.float32), 1, 'share_stats')
+        norm, acts = lax.optimization_barrier((norm, acts))
         mine = lax.dynamic_slice_in_dim(acts, stage_id * half, half)
         far = other(lax.dynamic_slice_in_dim(acts, (1 - stage_id) * half, half))
         act0, act1 = by_stage(mine, far)
-
-        def blocks(*tiles):
-            return jnp.stack([jnp.asarray(t, jnp.int32) for t in tiles])
-
-        shard = blocks(dev_id * n_wide, rest0 + dev_id * n_rest - n_wide)
-        stat = head_stats(z_all, embed_table, shard, n_wide, n_tiles)
-        stats = lax.all_gather(stat, BOTH, axis=0, tiled=False)
-        top = jnp.max(stats[:, 0], axis=0)
-        total = jnp.sum(stats[:, 1] * jnp.exp(stats[:, 0] - top[None]), axis=0)
-        norm = jnp.stack([top, 1.0 / total])
         g_shard, d_top_part = head_grads(z_all, norm, tgts, embed_table, grad_embed, shard, n_wide, n_tiles, n_rep, True)
-        d_top_part, act0, act1 = lax.optimization_barrier((d_top_part, act0, act1))
         d_top_own = lax.psum_scatter(d_top_part, BOTH, scatter_dimension=0, tiled=True)
         red_tile = rest0 + stage_id * n_red
         g_own = head_grads(z_all, norm, tgts, embed_table, grad_embed, blocks(red_tile, red_tile), n_red, n_red, n_rep, False)[0]
         d_top_own, g_own = lax.optimization_barrier((d_top_own, g_own))
-        d_top_own = d_top_own.reshape(d_model, -1).T.astype(jnp.bfloat16)
+        d_top_own = d_top_own.reshape(-1, d_model).astype(jnp.bfloat16)
+        g_shard, d_top_own, late_ids = lax.optimization_barrier((g_shard, d_top_own, ids))
         d_top = lax.all_gather(d_top_own, BOTH, axis=0, tiled=True)
-        g_shard, d_top_own = lax.optimization_barrier((g_shard, d_top_own))
+        sorted_ids = jnp.sum(jnp.where(rank[None, :] == order[:, None], late_ids[None, :], 0), axis=1).reshape(n_tok // SEG, SEG)
+        d_top, sorted_ids = lax.optimization_barrier((d_top, sorted_ids))
         g_far = other(g_own)
         g_wide = lax.all_gather(g_shard, BOTH, axis=0, tiled=True)
 
@@ -488,8 +557,9 @@
         embed_sq = (jnp.sum(rows_sumsq(blocks(dev_id * n_wide, 0), starts, sorted_ids, low, g_shard, n_wide, low_scale))
                     + jnp.sum(rows_sumsq(blocks(red_tile + my_part, my_part), starts, sorted_ids, low, g_own, n_part, low_scale)))
         stage_sq = jnp.sum(full_first * full_first) + jnp.sum(full_second * full_second)
-        parts_sq = lax.all_gather(jnp.full((1, 128), embed_sq + stage_sq / n_rep), BOTH, axis=0, tiled=True)
-        total_sq = jnp.sum(parts_sq[:, 0])
+        own_sq = jnp.full((8, 128), embed_sq + stage_sq / n_rep)
+        all_sq = small_exchange(gather_kernel, own_sq, jax.ShapeDtypeStruct((n_dev, 8, 128), jnp.float32), 2, 'share_sums')
+        total_sq = jnp.sum(all_sq[:, 0, 0])
         clip_scale = jnp.minimum(1.0, max_norm[0] / (jnp.sqrt(total_sq) + CLIP_EPS))
         new_first, new_mom_first, new_vel_first = adamw_update(w_first[0], mom_first[0], vel_first[0], full_first, clip_scale)
         new_second, new_mom_second, new_vel_second = adamw_update(w_second[0], mom_second[0], vel_second[0], full_second, clip_scale)

time: 887 us -> 815 us (0.919)
  blocking collectives: 46.2 us -> 10 us
  waiting for transfers between devices: 45.3 us -> 29 us
  Pallas kernels: 578 us -> 562 us
    pallas_call x2, Pallas kernels: 127 us -> 99.4 us  [next_forward(): pl.pallas_call(functools.partial(next_kernel, scale, n_tok // TOKEN_BLOCK...]
    unnamed x1 -> x0, blocking collectives: 23.1 us -> none
    all_gather x1, waiting for transfers between devices: 20.3 us -> 0.01 us  [local_step(): d_top = lax.all_gather(d_top_own, BOTH, axis=0, tiled=True)]
    pallas_call x0 -> x2, Pallas kernels: none -> 17 us  [small_exchange(): pl.pallas_call(body, out_shape=out_shape, in_specs=[pl.BlockSpec(memory_s...]
    all_gather x1 -> x0, blocking collectives: 13 us -> none  [local_step(): stats = lax.all_gather(stat, BOTH, axis=0, tiled=False)]
    optimization_barrier x1 -> x0, local copies, waits for them, and re-layouts: 9.12 us -> none  [local_step(): d_top_part, act0, act1 = lax.optimization_barrier((d_top_part, act0, act1))]
  transfers between devices with their start and end apart: 19 -> 19, of which waited for: 5 -> 4; matrix products, arithmetic and copies ran while one was open for 13% -> 16% of each run, Pallas kernels for 38% -> 33%
where the time goes in v2:
time: 815 us; the launch traced here: 808 us
  Pallas kernels  562 us (69%)
  other arithmetic  133 us (16%)
  waiting for transfers between devices  29 us (4%)
  starting transfers between devices  20.2 us (2%)
  matrix products  19 us (2%)
  between operations  18.6 us (2%)
  local copies, waits for them, and re-layouts  17.1 us (2%)
  blocking collectives  10 us (1%)
    pallas_call x1, Pallas kernels, embed_adam(): pl.pallas_call(functools.partial(adam_kernel, low_scale, n_wide, n_red),...  171 us
    pallas_call x2, Pallas kernels, head_grads(): pl.pallas_call(functools.partial(head_kernel, vocab, n_chunks, n_rep, n_o...  147 us
    pallas_call x2, Pallas kernels, next_forward(): pl.pallas_call(functools.partial(next_kernel, scale, n_tok // TOKEN_BLOCK...  99.4 us
    pallas_call x2, Pallas kernels, block_backward(): pl.pallas_call(functools.partial(backward_kernel, n_chunks), out_shape=[j...  75.5 us
    pallas_call x1, Pallas kernels, head_stats(): pl.pallas_call(functools.partial(stats_kernel, vocab, n_tok // CHUNK, n_o...  35.1 us
    select_n x5, other arithmetic, by_stage(): return (jnp.where(low_core, own, far), jnp.where(low_core, far, own))  22.3 us
    reduce_sum x1, other arithmetic, local_step(): rank = jnp.sum(before.astype(jnp.int32), axis=1)  19.7 us
    all_gather x2, waiting for transfers between devices, local_step(): lax.all_gather(final_act.reshape(my_micro // 2, tokens, d_model), 'stage'...  18.1 us
  transfers between devices with their start and end apart: 19, of which 4 were waited for; matrix products, arithmetic and copies ran while one was open for 16% of the time, Pallas kernels for 33%

profile of v2, /device:TPU:0, one launch (start us, length us, event | category | flops | bytes accessed | tf_op | source)
XLA Modules:
  0.0 808.1 jit_solution(6349365464522369104)
XLA Ops:
  7.2 2.5 bitcast_convert_fusion
  9.8 7.9 add_convert_fusion
  18.8 1.3 collective-permute-start
  20.1 2.5 collective-permute-done
  22.6 1.9 slice_select_fusion
  24.6 10.0 %all_gather.22 = s32[2,4096]{1,0:T(2,128)S(1)} all-gather(s32[2,1024]{1,0:T(2,128)S(1)} %pad_add_fusion), channel_id=1, replica_groups=mesh['data'=4,'stage'=2] {'data'}, dimensions={1}, use_global_device_ids=true | all-gather | bytes 40960 | tf_op jit(solution)/shard_map/all_gather | solution.py:504
  36.1 19.7 %convert_reduce_fusion = s32[4096]{0:T(1024)S(1)} fusion(s32[4096]{0:T(1024)S(1)} %bitcast.121), kind=kLoop, calls=%fused_computation.2 | loop fusion | flops 117436416 | bytes 32768 | tf_op jit(solution)/shard_map/reduce_sum | solution.py:512
  55.8 2.5 all-gather.7.cloned.1.call-done.z_ref
  59.1 35.1 %head_stats.1.x_ref = f32[2,4096]{1,0:T(2,128)} custom-call(s32[2]{0:T(128)} %pad_add_fusion.2.blk_ref, bf16[4096,512]{1,0:T(8,128)(2,1)} %all-gather.7.cloned.1.call-done.z_ref, f32[32128,512]{1,0:T(8,128)} %w_ref.1), custom_call_target="tpu_custom_call" | custom-call | flops 17179869184 | bytes 8388608 | tf_op jit(solution)/shard_map/head_stats/pallas_call | solution.py:157
  94.2 10.1 %share_stats.1.norm_ref = f32[2,4096]{1,0:T(2,128)} custom-call(f32[2,4096]{1,0:T(2,128)} %head_stats.1.x_ref), custom_call_target="tpu_custom_call" | custom-call | tf_op jit(solution)/shard_map/share_stats/pallas_call | solution.py:455
  104.3 5.2 all-gather.9.cloned.1.call-done
  109.5 73.3 %head_grads.1 = (f32[2560,512]{1,0:T(8,128)}, f32[8,512,512]{2,1,0:T(8,128)}) custom-call(s32[2]{0:T(128)} %pad_add_fusion.2.blk_ref, bf16[4096,512]{1,0:T(8,128)(2,1)} %all-gather.7.cloned.1.call-done.z_ref, f32[2,4096]{1,0:T(2,128)} %share_stats.1.norm_ref, s32[1,4096]{1,0:T(1,128)} %get-tuple-element.82.tgt_ref, f32[32128,512]{1,0:T(8,128)} %w_ref.1, ...), custom_call_target="tpu_custom_call" | custom-call | flops 51539607552 | bytes 25165824 | tf_op jit(solution)/shard_map/head_grads/pallas_call | solution.py:224
  183.5 73.4 %head_rows.1.g_ref.go_ref = f32[6144,512]{1,0:T(8,128)} custom-call(s32[2]{0:T(128)} %pad_add_fusion.3.blk_ref, bf16[4096,512]{1,0:T(8,128)(2,1)} %all-gather.7.cloned.1.call-done.z_ref, f32[2,4096]{1,0:T(2,128)} %share_stats.1.norm_ref, s32[1,4096]{1,0:T(1,128)} %get-tuple-element.82.tgt_ref, f32[32128,512]{1,0:T(8,128)} %w_ref.1, f32[32128,512]{1,0:T(8,128)} %g_ref.3), custom_call_target="tpu_custom_call" | custom-call | flops 51539607552 | bytes 37748736 | tf_op jit(solution)/shard_map/head_rows/pallas_call | solution.py:224
  256.9 2.1 convert_bitcast_fusion
  259.9 3.8 bitcast_convert_fusion.1
  264.2 3.0 constant_dynamic-slice_fusion
  267.3 5.4 broadcast_select_fusion.6
  272.6 4.2 broadcast_select_fusion.2
  276.9 4.4 broadcast_select_fusion.7
  281.3 9.9 %select_reduce_fusion = s32[4096]{0:T(1024)S(1)} fusion(s32[4096]{0:T(1024)S(1)} %bitcast.122, s32[4096]{0:T(1024)S(1)} %convert_reduce_fusion), kind=kLoop, calls=%fused_computation | loop fusion | flops 50327552 | bytes 49152 | tf_op jit(solution)/shard_map/reduce_sum | solution.py:537
  291.9 3.0 constant_dynamic-slice_fusion.1.g_ref
  294.9 37.8 %block_backward.2 = (bf16[2048,512]{1,0:T(8,128)(2,1)}, f32[512,2048]{1,0:T(8,128)}, f32[2048,512]{1,0:T(8,128)}) custom-call(bf16[2048,512]{1,0:T(8,128)(2,1)} %constant_dynamic-slice_fusion.1.g_ref, bf16[2048,512]{1,0:T(8,128)(2,1)} %get-tuple-element.71.x_ref, bf16[512,2048]{1,0:T(8,128)(2,1)} %get-tuple-element.79.wi_ref, ...), custom_call_target="tpu_custom_call" | custom-call | flops 21474836480 | bytes 12582912 | tf_op jit(solution)/shard_map/block_backward/pallas_call | solution.py:88
  332.7 37.8 %block_backward.3 = (bf16[2048,512]{1,0:T(8,128)(2,1)}, f32[512,2048]{1,0:T(8,128)}, f32[2048,512]{1,0:T(8,128)}) custom-call(bf16[2048,512]{1,0:T(8,128)(2,1)} %get-tuple-element.47.g_ref, bf16[2048,512]{1,0:T(8,128)(2,1)} %get-tuple-element.70.x_ref, bf16[512,2048]{1,0:T(8,128)(2,1)} %get-tuple-element.78.wi_ref, bf16[2048,512]{1,0:T(8,128)(2,1)} %get-tuple-element.76.wo_ref), custom_call_target="tpu_custom_call" | custom-call | flops 21474836480 | bytes 12582912 | tf_op jit(solution)/shard_map/block_backward/pallas_call | solution.py:88
  370.4 11.1 %fusion.12 = bf16[4096,512]{1,0:T(8,128)(2,1)S(1)} fusion(bf16[2048,512]{1,0:T(8,128)(2,1)} %get-tuple-element.48, s32[2048]{0:T(1024)S(1)} %dynamic-slice-done), kind=kOutput, calls=%fused_computation.21 | convolution fusion | flops 8600420352 | bytes 6299648 | tf_op jit(solution)/shard_map/dot_general | solution.py:547
  381.5 2.0 copy-done.6
  384.0 1.3 collective-permute-start.7
  385.3 7.0 collective-permute-start.8
  392.3 1.3 collective-permute-start.5
  393.6 2.0 copy-done.7
  395.6 7.0 collective-permute-start.6
  403.9 6.7 add.109.low_ref
  410.6 7.1 rows_sumsq.3
  417.7 9.5 %rows_sumsq.2 = f32[8,512]{1,0:T(8,128)} custom-call(s32[2]{0:T(128)} %get-tuple-element.84.blk_ref, s32[65]{0:T(128)} %convert_reduce_fusion.1.start_ref, s32[16,256]{1,0:T(8,128)} %reshape.53.ids_ref, bf16[4096,512]{1,0:T(8,128)(2,1)} %add.109.low_ref, f32[2560,512]{1,0:T(8,128)} %get-tuple-element.49.g_ref), custom_call_target="tpu_custom_call" | custom-call | tf_op jit(solution)/shard_map/rows_sumsq/pallas_call | solution.py:269
  427.8 1.3 reduce_sum.75
  429.1 12.8 %multiply_reduce_fusion = (f32[]{:T(128)}, f32[2048,512]{1,0:T(8,128)}) fusion(f32[2048,512]{1,0:T(8,128)} %get-tuple-element.54, f32[2048,512]{1,0:T(8,128)} %collective-permute-done.8, f32[2048,512]{1,0:T(8,128)} %get-tuple-element.53, f32[2048,512]{1,0:T(8,128)} %collective-permute-done.7, pred[]{:T(512)S(6)} %eq.14, f32[1,2048,512]{2,1,0:T(8,128)} %param.24), kind=kLoop, calls=%fused_computation.38 | loop fusion | flops 7340031 | bytes 25165828 | tf_op jit(solution)/shard_map/reduce_sum | solution.py:559
  442.0 10.9 %multiply_reduce_fusion.1 = (f32[]{:T(128)}, f32[512,2048]{1,0:T(8,128)}) fusion(f32[512,2048]{1,0:T(8,128)} %get-tuple-element.52, f32[512,2048]{1,0:T(8,128)} %collective-permute-done.6, f32[512,2048]{1,0:T(8,128)} %get-tuple-element.51, f32[512,2048]{1,0:T(8,128)} %collective-permute-done.5, pred[]{:T(512)S(6)} %eq.14, f32[1,512,2048]{2,1,0:T(8,128)S(1)} %copy-done.3), kind=kLoop, calls=%fused_computation.39 | loop fusion | flops 7340031 | bytes 25165828 | tf_op jit(solution)/shard_map/reduce_sum | solution.py:559
  456.1 6.9 share_sums.1
  463.0 1.4 slice_reduce_fusion
  465.1 11.3 %fusion.42 = (bf16[2048,512]{1,0:T(8,128)(2,1)S(1)}, f32[2048,512]{1,0:T(8,128)}, f32[1,2048,512]{2,1,0:T(8,128)}, f32[1,2048,512]{2,1,0:T(8,128)}) fusion(f32[1,2048,512]{2,1,0:T(8,128)} %param.22, f32[2048,512]{1,0:T(8,128)} %get-tuple-element.63, f32[]{:T(128)} %min.3, f32[1,2048,512]{2,1,0:T(8,128)} %param.20, f32[1,2048,512]{2,1,0:T(8,128)} %param.18), kind=kLoop, calls=%fused_computation.80 | loop fusion | flops 17825792 | bytes 31457284 | tf_op jit(solution)/shard_map/convert_element_type | solution.py:569
  479.0 1.2 copy-done.5
  480.2 8.8 %fusion.43 = (bf16[512,2048]{1,0:T(8,128)(2,1)}, f32[512,2048]{1,0:T(8,128)}, f32[1,512,2048]{2,1,0:T(8,128)}, f32[1,512,2048]{2,1,0:T(8,128)}) fusion(f32[1,512,2048]{2,1,0:T(8,128)S(1)} %copy-done.4, f32[512,2048]{1,0:T(8,128)S(1)} %copy-done.2, f32[]{:T(128)} %min.3, f32[1,512,2048]{2,1,0:T(8,128)S(1)} %copy-done.5, f32[1,512,2048]{2,1,0:T(8,128)S(1)} %copy-done.1), kind=kLoop, calls=%fused_computation.81 | loop fusion | flops 17825792 | bytes 31457284 | tf_op jit(solution)/shard_map/convert_element_type | solution.py:569
  490.0 3.8 broadcast_select_fusion.4
  493.8 4.5 broadcast_select_fusion
  498.3 171.2 %embed_adam.1 = (f32[32128,512]{1,0:T(8,128)}, f32[32128,512]{1,0:T(8,128)}, f32[32128,512]{1,0:T(8,128)}) custom-call(s32[65]{0:T(128)} %convert_reduce_fusion.1.start_ref, s32[1]{0:T(128)} %bitcast.26.stage_ref, f32[1]{0:T(128)} %bitcast.27.clip_ref, s32[16,256]{1,0:T(8,128)} %reshape.53.ids_ref, bf16[4096,512]{1,0:T(8,128)(2,1)} %add.109.low_ref, ...), custom_call_target="tpu_custom_call" | custom-call | flops 328990720 | bytes 460587008 | tf_op jit(solution)/shard_map/embed_adam/pallas_call | solution.py:335
  669.5 49.6 %next_forward.2 = bf16[4096,512]{1,0:T(8,128)(2,1)} custom-call(s32[4096]{0:T(1024)} %get-tuple-element.87.ids_ref, f32[32128,512]{1,0:T(8,128)} %get-tuple-element.30.table_ref, bf16[512,2048]{1,0:T(8,128)(2,1)} %get-tuple-element.75.wi0_ref, bf16[2048,512]{1,0:T(8,128)(2,1)} %get-tuple-element.73.wo0_ref, bf16[512,2048]{1,0:T(8,128)(2,1)} %get-tuple-element.74.wi1_ref, ...), custom_call_target="tpu_custom_call" | custom-call | flops 34359738368 | bytes 12582912 | tf_op jit(solution)/shard_map/next_forward/pallas_call | solution.py:397
  719.2 49.8 %next_forward.3 = bf16[4096,512]{1,0:T(8,128)(2,1)} custom-call(s32[4096]{0:T(1024)} %get-tuple-element.86.ids_ref, f32[32128,512]{1,0:T(8,128)} %get-tuple-element.30.table_ref, bf16[512,2048]{1,0:T(8,128)(2,1)} %get-tuple-element.75.wi0_ref, bf16[2048,512]{1,0:T(8,128)(2,1)} %get-tuple-element.73.wo0_ref, bf16[512,2048]{1,0:T(8,128)(2,1)} %get-tuple-element.74.wi1_ref, ...), custom_call_target="tpu_custom_call" | custom-call | flops 34359738368 | bytes 12582912 | tf_op jit(solution)/shard_map/next_forward/pallas_call | solution.py:397
  769.1 18.1 %all-gather.17.cloned.1.call-done = bf16[2,4,1024,512]{3,2,1,0:T(8,128)(2,1)} async-done(((bf16[1,4,1024,512]{3,2,1,0:T(8,128)(2,1)}), bf16[2,4,1024,512]{3,2,1,0:T(8,128)(2,1)}) %all-gather.17.cloned.1.call-update) | async-done | bytes 8388624 | tf_op jit(solution)/shard_map/all_gather | solution.py:578
  787.2 13.8 %pad_maximum_fusion = bf16[2,2,4,1024,512]{4,3,2,1,0:T(8,128)(2,1)} fusion(bf16[2,1,4,1024,512]{4,3,2,1,0:T(8,128)(2,1)} %bitcast.114, bf16[2,1,4,1024,512]{4,3,2,1,0:T(8,128)(2,1)} %bitcast.113), kind=kLoop, calls=%fused_computation.8 | loop fusion | flops 8388608 | bytes 33554432 | tf_op jit(solution)/shard_map/stack | solution.py:579
  (78 shorter events, 12.2 us)
Async XLA Ops:
  7.2 2.6 copy-start.9
  7.2 51.1 %all-gather.7.cloned.1.call-start = ((), (), s32[]{:S(2)}) async-start(), calls=%async_computation.1 | async-start | bytes 4718592 | tf_op jit(solution)/shard_map/all_gather | solution.py:508
  9.8 14.8 %copy-start.13 = (s32[1024]{0:T(1024)S(1)}, s32[1024]{0:T(1024)}, u32[]{:S(2)}) copy-start(s32[1024]{0:T(1024)} %param.31) | copy-start | bytes 12292
  9.8 14.8 %copy-start.14 = (s32[1024]{0:T(1024)S(1)}, s32[1024]{0:T(1024)}, u32[]{:S(2)}) copy-start(s32[1024]{0:T(1024)} %param.30) | copy-start | bytes 12292
  18.8 3.8 collective-permute-start
  24.5 85.0 %all-gather.9.cloned.1.call-start = ((), (), s32[]{:S(2)}) async-start(), calls=%async_computation.2 | async-start | bytes 5242880 | tf_op jit(solution)/shard_map/all_gather | solution.py:517
  55.8 225.5 %copy-start.12 = (s32[4096]{0:T(1024)}, s32[4096]{0:T(1024)S(1)}, u32[]{:S(2)}) copy-start(s32[4096]{0:T(1024)S(1)} %convert_reduce_fusion) | copy-start | bytes 49156
  58.3 198.6 %reduce-scatter.2.cloned.1.call-start = ((), (), s32[]{:S(2)}) async-start(), calls=%async_computation.3 | async-start | bytes 9437184 | tf_op jit(solution)/shard_map/reduce_scatter | solution.py:530
  182.8 109.0 %all-gather.11.cloned.1.call-start = ((), (), s32[]{:S(2)}) async-start(), calls=%async_computation.4 | async-start | bytes 4718592 | tf_op jit(solution)/shard_map/all_gather | solution.py:536
  259.0 239.3 %all-gather.13.cloned.1.call-start = ((), (), s32[]{:S(2)}) async-start(), calls=%async_computation.5 | async-start | bytes 47185920 | tf_op jit(solution)/shard_map/all_gather | solution.py:540
  259.6 509.5 %all-gather.15.cloned.1.call-start = ((), (), s32[]{:S(2)}) async-start(), calls=%async_computation.6 | async-start | bytes 12582912 | tf_op jit(solution)/shard_map/all_gather | solution.py:578
  259.9 7.4 collective-permute-start.3
  263.7 8.9 %collective-permute-start.2 = (bf16[512,2048]{1,0:T(8,128)(2,1)}, bf16[512,2048]{1,0:T(8,128)(2,1)}, u32[]{:S(2)}, u32[]{:S(2)}) collective-permute-start(bf16[512,2048]{1,0:T(8,128)(2,1)} %bitcast_convert_fusion.1), channel_id=1, source_target_pairs={{0,1},{1,0},{2,3},{3,2},{4,5},{5,4},{6,7},{7,6}} | collective-permute-start | bytes 6291464 | tf_op jit(solution)/shard_map/ppermute | solution.py:492
  267.3 9.6 %collective-permute-start.1 = (bf16[2048,512]{1,0:T(8,128)(2,1)}, bf16[2048,512]{1,0:T(8,128)(2,1)}, u32[]{:S(2)}, u32[]{:S(2)}) collective-permute-start(bf16[2048,512]{1,0:T(8,128)(2,1)} %constant_dynamic-slice_fusion), channel_id=1, source_target_pairs={{0,1},{1,0},{2,3},{3,2},{4,5},{5,4},{6,7},{7,6}} | collective-permute-start | bytes 6291464 | tf_op jit(solution)/shard_map/ppermute | solution.py:492
  267.3 5.4 copy-start
  272.6 4.3 copy-start.8
  332.7 37.8 %dynamic-slice-start = ((s32[4096]{0:T(1024)}, s32[]{:T(128)}), s32[2048]{0:T(1024)S(1)}, s32[]{:S(2)}) async-start(s32[4096]{0:T(1024)} %copy-done.12, s32[]{:T(128)} %select_n.86), calls=%async_computation.8 | async-start | bytes 16896 | tf_op jit(solution)/shard_map/dynamic_slice | solution.py:545
  381.5 2.0 copy-start.6
  383.5 10.1 %collective-permute-start.4 = (bf16[4096,512]{1,0:T(8,128)(2,1)S(1)}, bf16[4096,512]{1,0:T(8,128)(2,1)S(1)}, u32[]{:S(2)}, u32[]{:S(2)}) collective-permute-start(bf16[4096,512]{1,0:T(8,128)(2,1)S(1)} %fusion.12), channel_id=1, source_target_pairs={{0,1},{1,0},{2,3},{3,2},{4,5},{5,4},{6,7},{7,6}} | collective-permute-start | bytes 12582920 | tf_op jit(solution)/shard_map/ppermute | solution.py:492
  384.0 114.3 %collective-permute-start.9 = (f32[6144,512]{1,0:T(8,128)}, f32[6144,512]{1,0:T(8,128)}, u32[]{:S(2)}, u32[]{:S(2)}) collective-permute-start(f32[6144,512]{1,0:T(8,128)} %head_rows.1.g_ref.go_ref), channel_id=1, source_target_pairs={{0,1},{1,0},{2,3},{3,2},{4,5},{5,4},{6,7},{7,6}} | collective-permute-start | bytes 37748744 | tf_op jit(solution)/shard_map/ppermute | solution.py:492
  384.0 45.1 %collective-permute-start.7 = (f32[2048,512]{1,0:T(8,128)}, f32[2048,512]{1,0:T(8,128)}, u32[]{:S(2)}, u32[]{:S(2)}) collective-permute-start(f32[2048,512]{1,0:T(8,128)} %get-tuple-element.53), channel_id=1, source_target_pairs={{1,0},{3,2},{5,4},{7,6}} | collective-permute-start | bytes 12582920 | tf_op jit(solution)/shard_map/ppermute | solution.py:551
  385.3 43.8 %collective-permute-start.8 = (f32[2048,512]{1,0:T(8,128)}, f32[2048,512]{1,0:T(8,128)}, u32[]{:S(2)}, u32[]{:S(2)}) collective-permute-start(f32[2048,512]{1,0:T(8,128)} %get-tuple-element.54), channel_id=1, source_target_pairs={{0,1},{2,3},{4,5},{6,7}} | collective-permute-start | bytes 12582920 | tf_op jit(solution)/shard_map/ppermute | solution.py:551
  392.3 49.7 %collective-permute-start.5 = (f32[512,2048]{1,0:T(8,128)}, f32[512,2048]{1,0:T(8,128)}, u32[]{:S(2)}, u32[]{:S(2)}) collective-permute-start(f32[512,2048]{1,0:T(8,128)} %get-tuple-element.51), channel_id=1, source_target_pairs={{1,0},{3,2},{5,4},{7,6}} | collective-permute-start | bytes 12582920 | tf_op jit(solution)/shard_map/ppermute | solution.py:551
  393.6 2.0 copy-start.7
  395.6 46.4 %collective-permute-start.6 = (f32[512,2048]{1,0:T(8,128)}, f32[512,2048]{1,0:T(8,128)}, u32[]{:S(2)}, u32[]{:S(2)}) collective-permute-start(f32[512,2048]{1,0:T(8,128)} %get-tuple-element.52), channel_id=1, source_target_pairs={{0,1},{2,3},{4,5},{6,7}} | collective-permute-start | bytes 12582920 | tf_op jit(solution)/shard_map/ppermute | solution.py:551
  417.7 9.5 %copy-start.10 = (f32[8,512]{1,0:T(8,128)S(1)}, f32[8,512]{1,0:T(8,128)}, u32[]{:S(2)}) copy-start(f32[8,512]{1,0:T(8,128)} %rows_sumsq.3) | copy-start | bytes 49156
  429.1 12.9 %copy-start.3 = (f32[1,512,2048]{2,1,0:T(8,128)S(1)}, f32[1,512,2048]{2,1,0:T(8,128)}, u32[]{:S(2)}) copy-start(f32[1,512,2048]{2,1,0:T(8,128)} %param.23) | copy-start | bytes 12582916
  465.1 11.7 %copy-start.1 = (f32[1,512,2048]{2,1,0:T(8,128)S(1)}, f32[1,512,2048]{2,1,0:T(8,128)}, u32[]{:S(2)}) copy-start(f32[1,512,2048]{2,1,0:T(8,128)} %param.17) | copy-start | bytes 12582916
  465.1 12.7 %copy-start.2 = (f32[512,2048]{1,0:T(8,128)S(1)}, f32[512,2048]{1,0:T(8,128)}, u32[]{:S(2)}) copy-start(f32[512,2048]{1,0:T(8,128)} %get-tuple-element.65) | copy-start | bytes 12582916
  465.1 13.9 %copy-start.4 = (f32[1,512,2048]{2,1,0:T(8,128)S(1)}, f32[1,512,2048]{2,1,0:T(8,128)}, u32[]{:S(2)}) copy-start(f32[1,512,2048]{2,1,0:T(8,128)} %param.21) | copy-start | bytes 12582916
  465.1 15.1 %copy-start.5 = (f32[1,512,2048]{2,1,0:T(8,128)S(1)}, f32[1,512,2048]{2,1,0:T(8,128)}, u32[]{:S(2)}) copy-start(f32[1,512,2048]{2,1,0:T(8,128)} %param.19) | copy-start | bytes 12582916
  476.4 13.5 %collective-permute-start.11 = (bf16[2048,512]{1,0:T(8,128)(2,1)S(1)}, bf16[2048,512]{1,0:T(8,128)(2,1)}, u32[]{:S(2)}, u32[]{:S(2)}) collective-permute-start(bf16[2048,512]{1,0:T(8,128)(2,1)S(1)} %get-tuple-element.58), channel_id=1, source_target_pairs={{0,1},{1,0},{2,3},{3,2},{4,5},{5,4},{6,7},{7,6}} | collective-permute-start | bytes 6291464 | tf_op jit(solution)/shard_map/ppermute | solution.py:492
  480.2 9.1 %copy-start.11 = (s32[16,1024]{1,0:T(8,128)S(1)}, s32[16,1024]{1,0:T(8,128)}, u32[]{:S(2)}) copy-start(s32[16,1024]{1,0:T(8,128)} %param.32) | copy-start | bytes 196612
  489.0 4.8 collective-permute-start.10
  719.1 68.1 %all-gather.17.cloned.1.call-start = ((), (), s32[]{:S(2)}) async-start(), calls=%async_computation.7 | async-start | bytes 12582912 | tf_op jit(solution)/shard_map/all_gather | solution.py:578
Sparse Core Ops, SparseCore 0:
  24.6 33.5 all-gather.6
  60.1 49.4 all-gather.8
  183.0 62.2 reduce-scatter.1
  259.1 30.7 all-gather.10
  292.2 191.8 all-gather.12
  719.3 17.9 all-gather.14
  769.2 17.9 all-gather.16

commit v3 on v2

--- a/solution.py
+++ b/solution.py
@@ -38,16 +38,32 @@
     return (act_in.astype(jnp.float32) + mlp_out).astype(jnp.bfloat16)
 
 
-def backward_kernel(n_chunks, g_ref, x_ref, wi_ref, wo_ref, dx_ref, dwi_ref, dwo_ref, back_ref, acc_i, acc_o):
+def backward_kernel(n_chunks, n_ff, n_rep, g_ref, x_ref, wi_ref, wo_ref, old_i_ref, old_o_ref, dx_ref, full_i_ref, full_o_ref, sq_ref,
+                    back_ref, part_ref, far_ref, send_sems, recv_sems):
     f = pl.program_id(0)
+    partner = (lax.axis_index('data'), 1 - lax.axis_index('stage'))
+
+    def copy(i, which):
+        return pltpu.make_async_remote_copy(
+            src_ref=part_ref.at[i, which], dst_ref=far_ref.at[i, which], send_sem=send_sems.at[i, which],
+            recv_sem=recv_sems.at[i, which], device_id=partner, device_id_type=MESH_ID)
+
+    @pl.when(f == 0)
+    def _():
+        barrier = pltpu.get_barrier_semaphore()
+        pl.semaphore_signal(barrier, inc=1, device_id=partner, device_id_type=MESH_ID)
+        pl.semaphore_wait(barrier, 1)
+        back_ref[...] = jnp.zeros_like(back_ref)
+
+    for i in range(n_ff - 1):
+        @pl.when(f == i + 1)
+        def _():
+            copy(i, 0).start()
+            copy(i, 1).start()
+
     wi = wi_ref[...]
     wi_flip = wi.T
-    acc_i[...] = jnp.zeros_like(acc_i)
-    acc_o[...] = jnp.zeros_like(acc_o)
-
-    @pl.when(f == 0)
-    def _():
-        back_ref[...] = jnp.zeros_like(back_ref)
+    part_ref[f] = jnp.zeros(part_ref.shape[1:], jnp.float32)
 
     def chunk(c, _):
         rows = pl.ds(pl.multiple_of(c * CHUNK, CHUNK), CHUNK)
@@ -60,44 +76,64 @@
         hidden = (pre * rise).astype(jnp.bfloat16)
         slope = rise + (0.5 * GELU_K) * pre * (1.0 - bend * bend) * (1.0 + (3.0 * GELU_A) * square)
         d_pre = (d_hidden * slope).astype(jnp.bfloat16)
-        acc_o[...] += jnp.dot(hidden, g, preferred_element_type=jnp.float32)
-        acc_i[...] += jnp.dot(d_pre, x, preferred_element_type=jnp.float32)
+        part_ref[f, 0] += jnp.dot(d_pre, x, preferred_element_type=jnp.float32)
+        part_ref[f, 1] += jnp.dot(hidden, g, preferred_element_type=jnp.float32)
         back_ref[c] += jnp.dot(wi, d_pre, preferred_element_type=jnp.float32)
         return 0
 
     lax.fori_loop(0, n_chunks, chunk, 0, unroll=2)
-    dwo_ref[...] = acc_o[...]
-    dwi_ref[...] = acc_i[...].T
-
-    @pl.when(f == pl.num_programs(0) - 1)
-    def _():
+
+    @pl.when(f == n_ff - 1)
+    def _():
+        sq_ref[...] = jnp.zeros_like(sq_ref)
+
         def last(c, _):
             rows = pl.ds(pl.multiple_of(c * CHUNK, CHUNK), CHUNK)
             dx_ref[rows, :] = (g_ref[rows, :].astype(jnp.float32) + back_ref[c].T).astype(jnp.bfloat16)
             return 0
+
+        def squares(x):
+            sq_ref[...] += jnp.sum((x * x).reshape(-1, 8, x.shape[1]), axis=0)
+
         lax.fori_loop(0, n_chunks, last, 0)
-
-
-def block_backward(d_out, act_in, w_in, w_out):
+        copy(n_ff - 1, 0).start()
+        copy(n_ff - 1, 1).start()
+        for i in range(n_ff):
+            part = pl.ds(i * FF_CHUNK, FF_CHUNK)
+            copy(i, 0).wait()
+            copy(i, 1).wait()
+            full_i = old_i_ref[:, part] + (part_ref[i, 0] + far_ref[i, 0]).T * (1.0 / n_rep)
+            full_i_ref[:, part] = full_i
+            squares(full_i)
+            full_o = old_o_ref[part, :] + (part_ref[i, 1] + far_ref[i, 1]) * (1.0 / n_rep)
+            full_o_ref[part, :] = full_o
+            squares(full_o)
+
+
+def block_backward(d_out, act_in, w_in, w_out, old_in, old_out, n_rep, collective_id):
     n_tok, d_model = act_in.shape
     ff = w_in.shape[1]
-    n_chunks = n_tok // CHUNK
-    tokens = pl.BlockSpec((n_tok, d_model), lambda f: (0, 0))
-    cols = pl.BlockSpec((d_model, FF_CHUNK), lambda f: (0, f))
-    rows = pl.BlockSpec((FF_CHUNK, d_model), lambda f: (f, 0))
-    return pl.pallas_call(
-        functools.partial(backward_kernel, n_chunks),
+    n_chunks, n_ff = n_tok // CHUNK, ff // FF_CHUNK
+
+    def whole(*shape):
+        return pl.BlockSpec(shape, lambda f: (0, 0), pipeline_mode=pl.Buffered(1))
+
+    tokens = whole(n_tok, d_model)
+    part = (n_ff, 2, FF_CHUNK, d_model)
+    return pl.pallas_call(
+        functools.partial(backward_kernel, n_chunks, n_ff, n_rep),
         out_shape=[jax.ShapeDtypeStruct((n_tok, d_model), jnp.bfloat16), jax.ShapeDtypeStruct((d_model, ff), jnp.float32),
-                   jax.ShapeDtypeStruct((ff, d_model), jnp.float32)],
-        grid=(ff // FF_CHUNK,),
-        in_specs=[tokens, tokens, cols, rows],
-        out_specs=[tokens, cols, rows],
-        scratch_shapes=[pltpu.VMEM((n_chunks, d_model, CHUNK), jnp.float32), pltpu.VMEM((FF_CHUNK, d_model), jnp.float32),
-                        pltpu.VMEM((FF_CHUNK, d_model), jnp.float32)],
-        compiler_params=params(),
+                   jax.ShapeDtypeStruct((ff, d_model), jnp.float32), jax.ShapeDtypeStruct((8, d_model), jnp.float32)],
+        grid=(n_ff,),
+        in_specs=[tokens, tokens, pl.BlockSpec((d_model, FF_CHUNK), lambda f: (0, f)), pl.BlockSpec((FF_CHUNK, d_model), lambda f: (f, 0)),
+                  whole(d_model, ff), whole(ff, d_model)],
+        out_specs=[tokens, whole(d_model, ff), whole(ff, d_model), whole(8, d_model)],
+        scratch_shapes=[pltpu.VMEM((n_chunks, d_model, CHUNK), jnp.float32), pltpu.VMEM(part, jnp.float32), pltpu.VMEM(part, jnp.float32),
+                        pltpu.SemaphoreType.DMA((n_ff, 2)), pltpu.SemaphoreType.DMA((n_ff, 2))],
+        compiler_params=params(collective_id=collective_id, has_side_effects=True),
         cost_estimate=pl.CostEstimate(flops=10 * n_tok * d_model * ff, bytes_accessed=12 * d_model * ff, transcendentals=0),
         name='block_backward',
-    )(d_out, act_in, w_in, w_out)
+    )(d_out, act_in, w_in, w_out, old_in, old_out)
 
 
 def adamw_update(master, moment, velocity, gradient, clip_scale):
@@ -209,6 +245,32 @@
                 rest[0][c] = top_ref[c].T
                 return 0
             lax.fori_loop(0, n_chunks, turn, 0)
+
+
+def head_rows(z_all, norm, targets, embed_table, grad_embed, blocks, n_own, first, n_tiles, n_rep, held=None):
+    vocab, d_model = embed_table.shape
+    n_tok = z_all.shape[0]
+    last = (vocab - 1) // TILE
+    rows = pl.BlockSpec((TILE, d_model), lambda j, b: (jnp.minimum(b[0] + j, last), 0))
+
+    def kernel(blk_ref, z_ref, norm_ref, tgt_ref, e_ref, g_ref, *rest):
+        head_kernel(vocab, n_tok // CHUNK, n_rep, n_own, False, blk_ref, z_ref, norm_ref, tgt_ref, e_ref, g_ref, *rest[-2:])
+
+    return pl.pallas_call(
+        kernel,
+        out_shape=jax.ShapeDtypeStruct((n_own * TILE, d_model), jnp.float32),
+        grid_spec=pltpu.PrefetchScalarGridSpec(
+            num_scalar_prefetch=1, grid=(n_tiles,),
+            in_specs=[pl.BlockSpec((n_tok, d_model), lambda j, b: (0, 0)),
+                      pl.BlockSpec((2, n_tok), lambda j, b: (0, 0)),
+                      pl.BlockSpec((1, n_tok), lambda j, b: (0, 0)), rows, rows] + [pl.BlockSpec(memory_space=pl.ANY)] * (held is not None),
+            out_specs=pl.BlockSpec((TILE, d_model), lambda j, b: (first + j, 0)),
+            scratch_shapes=[pltpu.VMEM((TILE, d_model), jnp.float32)]),
+        input_output_aliases={} if held is None else {6: 0},
+        compiler_params=params(),
+        cost_estimate=pl.CostEstimate(flops=4 * n_tiles * TILE * n_tok * d_model, bytes_accessed=n_tiles * TILE * d_model * 12, transcendentals=0),
+        name='head_rows',
+    )(blocks + first, z_all, norm, targets, embed_table, grad_embed, *([] if held is None else [held]))
 
 
 def head_grads(z_all, norm, targets, embed_table, grad_embed, blocks, n_own, n_tiles, n_rep, with_top):
@@ -529,34 +591,35 @@
         g_shard, d_top_part = head_grads(z_all, norm, tgts, embed_table, grad_embed, shard, n_wide, n_tiles, n_rep, True)
         d_top_own = lax.psum_scatter(d_top_part, BOTH, scatter_dimension=0, tiled=True)
         red_tile = rest0 + stage_id * n_red
-        g_own = head_grads(z_all, norm, tgts, embed_table, grad_embed, blocks(red_tile, red_tile), n_red, n_red, n_rep, False)[0]
+        red = blocks(red_tile, red_tile)
+        n_early = n_red - n_red // 4
+        g_own = head_rows(z_all, norm, tgts, embed_table, grad_embed, red, n_red, 0, n_early, n_rep)
         d_top_own, g_own = lax.optimization_barrier((d_top_own, g_own))
         d_top_own = d_top_own.reshape(-1, d_model).astype(jnp.bfloat16)
         g_shard, d_top_own, late_ids = lax.optimization_barrier((g_shard, d_top_own, ids))
         d_top = lax.all_gather(d_top_own, BOTH, axis=0, tiled=True)
         sorted_ids = jnp.sum(jnp.where(rank[None, :] == order[:, None], late_ids[None, :], 0), axis=1).reshape(n_tok // SEG, SEG)
-        d_top, sorted_ids = lax.optimization_barrier((d_top, sorted_ids))
+        g_own = head_rows(z_all, norm, tgts, embed_table, grad_embed, red, n_red, n_early, n_red - n_early, n_rep, g_own)
+        d_top, sorted_ids, g_own = lax.optimization_barrier((d_top, sorted_ids, g_own))
         g_far = other(g_own)
         g_wide = lax.all_gather(g_shard, BOTH, axis=0, tiled=True)
 
         d_half = lax.dynamic_slice_in_dim(d_top, stage_id * half, half)
-        d_act1, g_in1, g_out1 = block_backward(d_half, act1, w_in1, w_out1)
-        d_low_half, g_in0, g_out0 = block_backward(d_act1, act0, w_in0, w_out0)
+        olds = (grad_first[0], grad_second[0], n_rep)
+        d_act1, full_in1, full_out1, sq1 = block_backward(d_half, act1, w_in1, w_out1, *olds, 3)
+        d_low_half, full_in0, full_out0, sq0 = block_backward(d_act1, act0, w_in0, w_out0, *olds, 4)
         my_rank = lax.dynamic_slice_in_dim(rank, stage_id * half, half)
         perm = (my_rank[None, :] == order[:, None]).astype(jnp.bfloat16)
         low_half = jnp.dot(perm, d_low_half, preferred_element_type=jnp.float32).astype(jnp.bfloat16)
         low = low_half + other(low_half)
 
-        def both_halves(part0, part1):
-            far0, far1 = lax.ppermute(part0, 'stage', [(1, 0)]), lax.ppermute(part1, 'stage', [(0, 1)])
-            return jnp.where(low_core, part0 + far0, part1 + far1)
-
-        full_first = grad_first[0] + both_halves(g_in0, g_in1) / n_rep
-        full_second = grad_second[0] + both_halves(g_out0, g_out1) / n_rep
+        full_first = jnp.where(low_core, full_in0, full_in1)
+        full_second = jnp.where(low_core, full_out0, full_out1)
+
         my_part = lax.axis_index('data') * n_part
         embed_sq = (jnp.sum(rows_sumsq(blocks(dev_id * n_wide, 0), starts, sorted_ids, low, g_shard, n_wide, low_scale))
                     + jnp.sum(rows_sumsq(blocks(red_tile + my_part, my_part), starts, sorted_ids, low, g_own, n_part, low_scale)))
-        stage_sq = jnp.sum(full_first * full_first) + jnp.sum(full_second * full_second)
+        stage_sq = jnp.sum(jnp.where(low_core, sq0, sq1))
         own_sq = jnp.full((8, 128), embed_sq + stage_sq / n_rep)
         all_sq = small_exchange(gather_kernel, own_sq, jax.ShapeDtypeStruct((n_dev, 8, 128), jnp.float32), 2, 'share_sums')
         total_sq = jnp.sum(all_sq[:, 0, 0])

time: 815 us -> 806 us (0.989)
  other arithmetic: 133 us -> 110 us
  Pallas kernels: 562 us -> 584 us
  starting transfers between devices: 20.2 us -> 3.3 us
  waiting for transfers between devices: 29 us -> 42.2 us
    pallas_call x2 -> x4, Pallas kernels: 75.5 us -> 170 us  [the longest x2 92.5 us: block_backward(): pl.pallas_call(functools.partial(backward_kernel, n_chunks, n_ff, n_rep),...]
    pallas_call x2 -> x1, Pallas kernels: 147 us -> 73.3 us  [head_grads(): pl.pallas_call(functools.partial(head_kernel, vocab, n_chunks, n_rep, n_o...]
    reduce_sum x2 -> x1, other arithmetic: 23.8 us -> 0.6 us  [local_step(): stage_sq = jnp.sum(jnp.where(low_core, sq0, sq1))]
    ppermute x4 -> x0, starting transfers between devices: 16.5 us -> none  [the longest x2 14 us: both_halves(): lax.ppermute(part1, 'stage', [(0, 1)])]
  transfers between devices with their start and end apart: 19 -> 15, of which waited for: 4 -> 6; matrix products, arithmetic and copies ran while one was open for 16% -> 14% of each run, Pallas kernels for 33% -> 36%
where the time goes in v3:
time: 806 us; the launch traced here: 801 us
  Pallas kernels  584 us (72%)
  other arithmetic  110 us (14%)
  waiting for transfers between devices  42.2 us (5%)
  matrix products  19.8 us (2%)
  between operations  18.2 us (2%)
  local copies, waits for them, and re-layouts  13.4 us (2%)
  blocking collectives  10 us (1%)
    pallas_call x1, Pallas kernels, embed_adam(): pl.pallas_call(functools.partial(adam_kernel, low_scale, n_wide, n_red),...  172 us
    pallas_call x2, Pallas kernels, next_forward(): pl.pallas_call(functools.partial(next_kernel, scale, n_tok // TOKEN_BLOCK...  99.5 us
    pallas_call x2, Pallas kernels, block_backward(): pl.pallas_call(functools.partial(backward_kernel, n_chunks, n_ff, n_rep),...  92.5 us
    pallas_call x2, Pallas kernels, head_rows(): pl.pallas_call(kernel, out_shape=jax.ShapeDtypeStruct((n_own * TILE, d_mo...  77.9 us
    pallas_call x1, Pallas kernels, head_grads(): pl.pallas_call(functools.partial(head_kernel, vocab, n_chunks, n_rep, n_o...  73.3 us
    pallas_call x1, Pallas kernels, head_stats(): pl.pallas_call(functools.partial(stats_kernel, vocab, n_tok // CHUNK, n_o...  35.1 us
    select_n x5, other arithmetic, by_stage(): return (jnp.where(low_core, own, far), jnp.where(low_core, far, own))  22.3 us
    reduce_sum x1, other arithmetic, local_step(): rank = jnp.sum(before.astype(jnp.int32), axis=1)  19.7 us
  transfers between devices with their start and end apart: 15, of which 6 were waited for; matrix products, arithmetic and copies ran while one was open for 14% of the time, Pallas kernels for 36%

profile of v3, /device:TPU:0, one launch (start us, length us, event | category | flops | bytes accessed | tf_op | source)
XLA Modules:
  0.0 800.6 jit_solution(15861572253674348825)
XLA Ops:
  7.2 2.5 bitcast_convert_fusion
  9.8 7.9 add_convert_fusion
  17.7 1.1 slice.30
  18.8 1.3 collective-permute-start
  20.1 2.5 collective-permute-done
  22.6 1.9 slice_select_fusion
  24.6 10.0 %all_gather.22 = s32[2,4096]{1,0:T(2,128)S(1)} all-gather(s32[2,1024]{1,0:T(2,128)S(1)} %pad_add_fusion), channel_id=1, replica_groups=mesh['data'=4,'stage'=2] {'data'}, dimensions={1}, use_global_device_ids=true | all-gather | bytes 40960 | tf_op jit(solution)/shard_map/all_gather | solution.py:566
  34.6 0.6 fusion.42
  35.3 0.9 convert_reduce_fusion.1.start_ref
  36.1 19.7 %convert_reduce_fusion = s32[4096]{0:T(1024)S(1)} fusion(s32[4096]{0:T(1024)S(1)} %bitcast.101), kind=kLoop, calls=%fused_computation.2 | loop fusion | flops 117436416 | bytes 32768 | tf_op jit(solution)/shard_map/reduce_sum | solution.py:574
  55.8 2.5 all-gather.7.cloned.1.call-done.z_ref
  59.2 35.1 %head_stats.1.x_ref = f32[2,4096]{1,0:T(2,128)} custom-call(s32[2]{0:T(128)} %pad_add_fusion.2.blk_ref, bf16[4096,512]{1,0:T(8,128)(2,1)} %all-gather.7.cloned.1.call-done.z_ref, f32[32128,512]{1,0:T(8,128)} %w_ref.1), custom_call_target="tpu_custom_call" | custom-call | flops 17179869184 | bytes 8388608 | tf_op jit(solution)/shard_map/head_stats/pallas_call | solution.py:193
  94.3 10.1 %share_stats.1.norm_ref = f32[2,4096]{1,0:T(2,128)} custom-call(f32[2,4096]{1,0:T(2,128)} %head_stats.1.x_ref), custom_call_target="tpu_custom_call" | custom-call | tf_op jit(solution)/shard_map/share_stats/pallas_call | solution.py:517
  104.4 5.2 all-gather.9.cloned.1.call-done
  109.6 73.3 %head_grads.1 = (f32[2560,512]{1,0:T(8,128)}, f32[8,512,512]{2,1,0:T(8,128)}) custom-call(s32[2]{0:T(128)} %pad_add_fusion.2.blk_ref, bf16[4096,512]{1,0:T(8,128)(2,1)} %all-gather.7.cloned.1.call-done.z_ref, f32[2,4096]{1,0:T(2,128)} %share_stats.1.norm_ref, s32[1,4096]{1,0:T(1,128)} %get-tuple-element.84.tgt_ref, f32[32128,512]{1,0:T(8,128)} %w_ref.1, ...), custom_call_target="tpu_custom_call" | custom-call | flops 51539607552 | bytes 25165824 | tf_op jit(solution)/shard_map/head_grads/pallas_call | solution.py:286
  183.5 56.2 %head_rows.2.rest_0_ = f32[6144,512]{1,0:T(8,128)} custom-call(s32[2]{0:T(128)} %pad_add_fusion.3.blk_ref, bf16[4096,512]{1,0:T(8,128)(2,1)} %all-gather.7.cloned.1.call-done.z_ref, f32[2,4096]{1,0:T(2,128)} %share_stats.1.norm_ref, s32[1,4096]{1,0:T(1,128)} %get-tuple-element.84.tgt_ref, f32[32128,512]{1,0:T(8,128)} %w_ref.1, f32[32128,512]{1,0:T(8,128)} %g_ref.5), custom_call_target="tpu_custom_call" | custom-call | flops 38654705664 | bytes 28311552 | tf_op jit(solution)/shard_map/head_rows/pallas_call | solution.py:259
  239.7 5.6 reduce-scatter.2.cloned.1.call-done
  245.3 2.1 convert_bitcast_fusion
  248.1 3.8 bitcast_convert_fusion.1
  252.4 3.0 constant_dynamic-slice_fusion
  256.0 5.3 broadcast_select_fusion.6
  261.4 4.2 broadcast_select_fusion.2
  265.6 4.4 broadcast_select_fusion.7
  270.0 10.4 %select_reduce_fusion = s32[4096]{0:T(1024)S(1)} fusion(s32[4096]{0:T(1024)S(1)} %bitcast.102, s32[4096]{0:T(1024)S(1)} %convert_reduce_fusion), kind=kLoop, calls=%fused_computation | loop fusion | flops 50327552 | bytes 49152 | tf_op jit(solution)/shard_map/reduce_sum | solution.py:601
  281.0 21.7 %head_rows.3.g_ref.go_ref = f32[6144,512]{1,0:T(8,128)} custom-call(s32[2]{0:T(128)} %broadcast_add_fusion.blk_ref, bf16[4096,512]{1,0:T(8,128)(2,1)} %all-gather.7.cloned.1.call-done.z_ref, f32[2,4096]{1,0:T(2,128)} %share_stats.1.norm_ref, s32[1,4096]{1,0:T(1,128)} %get-tuple-element.84.tgt_ref, ...), custom_call_target="tpu_custom_call", output_to_operand_aliasing={{}: (6, {})} | custom-call | flops 12884901888 | bytes 9437184 | tf_op jit(solution)/shard_map/head_rows/pallas_call | solution.py:259
  303.2 3.0 constant_dynamic-slice_fusion.1.g_ref
  306.3 46.1 %block_backward.2 = (bf16[2048,512]{1,0:T(8,128)(2,1)}, f32[512,2048]{1,0:T(8,128)}, f32[2048,512]{1,0:T(8,128)}, f32[8,512]{1,0:T(8,128)}) custom-call(bf16[2048,512]{1,0:T(8,128)(2,1)} %constant_dynamic-slice_fusion.1.g_ref, bf16[2048,512]{1,0:T(8,128)(2,1)} %get-tuple-element.73.x_ref, bf16[512,2048]{1,0:T(8,128)(2,1)} %get-tuple-element.81.wi_ref, ...), custom_call_target="tpu_custom_call" | custom-call | flops 21474836480 | bytes 12582912 | tf_op jit(solution)/shard_map/block_backward/pallas_call | solution.py:123
  352.4 46.4 %block_backward.3 = (bf16[2048,512]{1,0:T(8,128)(2,1)}, f32[512,2048]{1,0:T(8,128)}, f32[2048,512]{1,0:T(8,128)}, f32[8,512]{1,0:T(8,128)}) custom-call(bf16[2048,512]{1,0:T(8,128)(2,1)} %get-tuple-element.51.g_ref, bf16[2048,512]{1,0:T(8,128)(2,1)} %get-tuple-element.72.x_ref, bf16[512,2048]{1,0:T(8,128)(2,1)} %get-tuple-element.80.wi_ref, ...), custom_call_target="tpu_custom_call" | custom-call | flops 21474836480 | bytes 12582912 | tf_op jit(solution)/shard_map/block_backward/pallas_call | solution.py:123
  398.8 11.9 %fusion.12 = bf16[4096,512]{1,0:T(8,128)(2,1)} fusion(bf16[2048,512]{1,0:T(8,128)(2,1)} %get-tuple-element.52, s32[2048]{0:T(1024)S(1)} %dynamic-slice-done), kind=kOutput, calls=%fused_computation.21 | convolution fusion | flops 8600420352 | bytes 6299648 | tf_op jit(solution)/shard_map/dot_general | solution.py:613
  413.4 7.3 collective-permute-done.4
  420.6 6.7 add.92.low_ref
  427.3 7.2 rows_sumsq.3
  434.5 9.5 %rows_sumsq.2 = f32[8,512]{1,0:T(8,128)} custom-call(s32[2]{0:T(128)} %get-tuple-element.86.blk_ref, s32[65]{0:T(128)} %convert_reduce_fusion.1.start_ref, s32[16,256]{1,0:T(8,128)} %reshape.53.ids_ref, bf16[4096,512]{1,0:T(8,128)(2,1)} %add.92.low_ref, f32[2560,512]{1,0:T(8,128)} %get-tuple-element.53.g_ref), custom_call_target="tpu_custom_call" | custom-call | tf_op jit(solution)/shard_map/rows_sumsq/pallas_call | solution.py:331
  444.6 1.3 reduce_sum.66
  447.8 6.7 share_sums.1
  454.5 1.4 slice_reduce_fusion
  456.7 11.1 %fusion.38 = (bf16[2048,512]{1,0:T(8,128)(2,1)S(1)}, f32[2048,512]{1,0:T(8,128)}, f32[2048,512]{1,0:T(8,128)}, f32[2048,512]{1,0:T(8,128)}) fusion(f32[1,2048,512]{2,1,0:T(8,128)} %param.18, f32[2048,512]{1,0:T(8,128)} %get-tuple-element.59, f32[2048,512]{1,0:T(8,128)} %get-tuple-element.60, pred[]{:T(512)S(6)} %eq.14, f32[]{:T(128)} %min.3, ...), kind=kLoop, calls=%fused_computation.76 | loop fusion | flops 18874368 | bytes 35651588 | tf_op jit(solution)/shard_map/convert_element_type | solution.py:632
  468.1 1.3 copy-done.2
  469.4 1.2 copy-done.3
  470.6 1.2 copy-done.4
  471.8 8.4 %fusion.40 = (bf16[512,2048]{1,0:T(8,128)(2,1)}, f32[512,2048]{1,0:T(8,128)}, f32[512,2048]{1,0:T(8,128)}, f32[512,2048]{1,0:T(8,128)}) fusion(f32[1,512,2048]{2,1,0:T(8,128)S(1)} %copy-done.1, f32[512,2048]{1,0:T(8,128)} %get-tuple-element.57, f32[512,2048]{1,0:T(8,128)S(1)} %copy-done.4, pred[]{:T(512)S(6)} %eq.14, f32[]{:T(128)} %min.3, ...), kind=kLoop, calls=%fused_computation.77 | loop fusion | flops 18874368 | bytes 35651588 | tf_op jit(solution)/shard_map/convert_element_type | solution.py:632
  480.8 3.8 broadcast_select_fusion.4
  484.7 4.5 broadcast_select_fusion
  489.2 172.1 %embed_adam.1 = (f32[32128,512]{1,0:T(8,128)}, f32[32128,512]{1,0:T(8,128)}, f32[32128,512]{1,0:T(8,128)}) custom-call(s32[65]{0:T(128)} %convert_reduce_fusion.1.start_ref, s32[1]{0:T(128)} %bitcast.26.stage_ref, f32[1]{0:T(128)} %bitcast.27.clip_ref, s32[16,256]{1,0:T(8,128)} %reshape.53.ids_ref, bf16[4096,512]{1,0:T(8,128)(2,1)} %add.92.low_ref, ...), custom_call_target="tpu_custom_call" | custom-call | flops 328990720 | bytes 460587008 | tf_op jit(solution)/shard_map/embed_adam/pallas_call | solution.py:397
  661.3 49.9 %next_forward.2 = bf16[4096,512]{1,0:T(8,128)(2,1)} custom-call(s32[4096]{0:T(1024)} %get-tuple-element.89.ids_ref, f32[32128,512]{1,0:T(8,128)} %get-tuple-element.33.table_ref, bf16[512,2048]{1,0:T(8,128)(2,1)} %get-tuple-element.77.wi0_ref, bf16[2048,512]{1,0:T(8,128)(2,1)} %get-tuple-element.75.wo0_ref, bf16[512,2048]{1,0:T(8,128)(2,1)} %get-tuple-element.76.wi1_ref, ...), custom_call_target="tpu_custom_call" | custom-call | flops 34359738368 | bytes 12582912 | tf_op jit(solution)/shard_map/next_forward/pallas_call | solution.py:459
  711.3 49.7 %next_forward.3 = bf16[4096,512]{1,0:T(8,128)(2,1)} custom-call(s32[4096]{0:T(1024)} %get-tuple-element.88.ids_ref, f32[32128,512]{1,0:T(8,128)} %get-tuple-element.33.table_ref, bf16[512,2048]{1,0:T(8,128)(2,1)} %get-tuple-element.77.wi0_ref, bf16[2048,512]{1,0:T(8,128)(2,1)} %get-tuple-element.75.wo0_ref, bf16[512,2048]{1,0:T(8,128)(2,1)} %get-tuple-element.76.wi1_ref, ...), custom_call_target="tpu_custom_call" | custom-call | flops 34359738368 | bytes 12582912 | tf_op jit(solution)/shard_map/next_forward/pallas_call | solution.py:459
  761.0 18.5 %all-gather.17.cloned.1.call-done = bf16[2,4,1024,512]{3,2,1,0:T(8,128)(2,1)} async-done(((bf16[1,4,1024,512]{3,2,1,0:T(8,128)(2,1)}), bf16[2,4,1024,512]{3,2,1,0:T(8,128)(2,1)}) %all-gather.17.cloned.1.call-update) | async-done | bytes 8388624 | tf_op jit(solution)/shard_map/all_gather | solution.py:641
  779.5 13.8 %pad_maximum_fusion = bf16[2,2,4,1024,512]{4,3,2,1,0:T(8,128)(2,1)} fusion(bf16[2,1,4,1024,512]{4,3,2,1,0:T(8,128)(2,1)} %bitcast.90, bf16[2,1,4,1024,512]{4,3,2,1,0:T(8,128)(2,1)} %bitcast.89), kind=kLoop, calls=%fused_computation.8 | loop fusion | flops 8388608 | bytes 33554432 | tf_op jit(solution)/shard_map/stack | solution.py:642
  (69 shorter events, 8.1 us)
Async XLA Ops:
  7.2 2.6 copy-start.6
  7.2 51.1 %all-gather.7.cloned.1.call-start = ((), (), s32[]{:S(2)}) async-start(), calls=%async_computation.1 | async-start | bytes 4718592 | tf_op jit(solution)/shard_map/all_gather | solution.py:570
  9.8 14.8 %copy-start.12 = (s32[1024]{0:T(1024)S(1)}, s32[1024]{0:T(1024)}, u32[]{:S(2)}) copy-start(s32[1024]{0:T(1024)} %param.31) | copy-start | bytes 12292
  9.8 14.8 %copy-start.13 = (s32[1024]{0:T(1024)S(1)}, s32[1024]{0:T(1024)}, u32[]{:S(2)}) copy-start(s32[1024]{0:T(1024)} %param.30) | copy-start | bytes 12292
  18.8 3.8 collective-permute-start
  24.5 85.1 %all-gather.9.cloned.1.call-start = ((), (), s32[]{:S(2)}) async-start(), calls=%async_computation.2 | async-start | bytes 5242880 | tf_op jit(solution)/shard_map/all_gather | solution.py:579
  55.8 214.2 %copy-start.11 = (s32[4096]{0:T(1024)}, s32[4096]{0:T(1024)S(1)}, u32[]{:S(2)}) copy-start(s32[4096]{0:T(1024)S(1)} %convert_reduce_fusion) | copy-start | bytes 49156
  58.3 187.0 %reduce-scatter.2.cloned.1.call-start = ((), (), s32[]{:S(2)}) async-start(), calls=%async_computation.3 | async-start | bytes 9437184 | tf_op jit(solution)/shard_map/reduce_scatter | solution.py:592
  182.9 119.9 %all-gather.11.cloned.1.call-start = ((), (), s32[]{:S(2)}) async-start(), calls=%async_computation.4 | async-start | bytes 4718592 | tf_op jit(solution)/shard_map/all_gather | solution.py:600
  247.4 241.8 %all-gather.13.cloned.1.call-start = ((), (), s32[]{:S(2)}) async-start(), calls=%async_computation.5 | async-start | bytes 47185920 | tf_op jit(solution)/shard_map/all_gather | solution.py:605
  248.0 513.0 %all-gather.15.cloned.1.call-start = ((), (), s32[]{:S(2)}) async-start(), calls=%async_computation.6 | async-start | bytes 12582912 | tf_op jit(solution)/shard_map/all_gather | solution.py:641
  248.0 8.0 collective-permute-start.3
  251.9 9.5 %collective-permute-start.2 = (bf16[512,2048]{1,0:T(8,128)(2,1)}, bf16[512,2048]{1,0:T(8,128)(2,1)}, u32[]{:S(2)}, u32[]{:S(2)}) collective-permute-start(bf16[512,2048]{1,0:T(8,128)(2,1)} %bitcast_convert_fusion.1), channel_id=1, source_target_pairs={{0,1},{1,0},{2,3},{3,2},{4,5},{5,4},{6,7},{7,6}} | collective-permute-start | bytes 6291464 | tf_op jit(solution)/shard_map/ppermute | solution.py:554
  255.4 10.2 %collective-permute-start.1 = (bf16[2048,512]{1,0:T(8,128)(2,1)}, bf16[2048,512]{1,0:T(8,128)(2,1)}, u32[]{:S(2)}, u32[]{:S(2)}) collective-permute-start(bf16[2048,512]{1,0:T(8,128)(2,1)} %constant_dynamic-slice_fusion), channel_id=1, source_target_pairs={{0,1},{1,0},{2,3},{3,2},{4,5},{5,4},{6,7},{7,6}} | collective-permute-start | bytes 6291464 | tf_op jit(solution)/shard_map/ppermute | solution.py:554
  256.0 5.4 copy-start
  261.4 4.3 copy-start.5
  302.7 186.4 %collective-permute-start.5 = (f32[6144,512]{1,0:T(8,128)}, f32[6144,512]{1,0:T(8,128)}, u32[]{:S(2)}, u32[]{:S(2)}) collective-permute-start(f32[6144,512]{1,0:T(8,128)} %head_rows.3.g_ref.go_ref), channel_id=1, source_target_pairs={{0,1},{1,0},{2,3},{3,2},{4,5},{5,4},{6,7},{7,6}} | collective-permute-start | bytes 37748744 | tf_op jit(solution)/shard_map/ppermute | solution.py:554
  352.4 46.4 %dynamic-slice-start = ((s32[4096]{0:T(1024)}, s32[]{:T(128)}), s32[2048]{0:T(1024)S(1)}, s32[]{:S(2)}) async-start(s32[4096]{0:T(1024)} %copy-done.11, s32[]{:T(128)} %select_n.94), calls=%async_computation.8 | async-start | bytes 16896 | tf_op jit(solution)/shard_map/dynamic_slice | solution.py:611
  398.8 13.3 %copy-start.9 = (f32[8,512]{1,0:T(8,128)S(1)}, f32[8,512]{1,0:T(8,128)}, u32[]{:S(2)}) copy-start(f32[8,512]{1,0:T(8,128)} %get-tuple-element.56) | copy-start | bytes 49156
  398.8 13.3 %copy-start.10 = (f32[8,512]{1,0:T(8,128)S(1)}, f32[8,512]{1,0:T(8,128)}, u32[]{:S(2)}) copy-start(f32[8,512]{1,0:T(8,128)} %get-tuple-element.55) | copy-start | bytes 49156
  410.7 9.9 %collective-permute-start.4 = (bf16[4096,512]{1,0:T(8,128)(2,1)}, bf16[4096,512]{1,0:T(8,128)(2,1)}, u32[]{:S(2)}, u32[]{:S(2)}) collective-permute-start(bf16[4096,512]{1,0:T(8,128)(2,1)} %fusion.12), channel_id=1, source_target_pairs={{0,1},{1,0},{2,3},{3,2},{4,5},{5,4},{6,7},{7,6}} | collective-permute-start | bytes 12582920 | tf_op jit(solution)/shard_map/ppermute | solution.py:554
  434.5 9.5 %copy-start.7 = (f32[8,512]{1,0:T(8,128)S(1)}, f32[8,512]{1,0:T(8,128)}, u32[]{:S(2)}) copy-start(f32[8,512]{1,0:T(8,128)} %rows_sumsq.3) | copy-start | bytes 49156
  456.6 11.5 %copy-start.1 = (f32[1,512,2048]{2,1,0:T(8,128)S(1)}, f32[1,512,2048]{2,1,0:T(8,128)}, u32[]{:S(2)}) copy-start(f32[1,512,2048]{2,1,0:T(8,128)} %param.17) | copy-start | bytes 12582916
  456.6 12.8 %copy-start.2 = (f32[1,512,2048]{2,1,0:T(8,128)S(1)}, f32[1,512,2048]{2,1,0:T(8,128)}, u32[]{:S(2)}) copy-start(f32[1,512,2048]{2,1,0:T(8,128)} %param.19) | copy-start | bytes 12582916
  456.7 14.0 %copy-start.3 = (f32[1,512,2048]{2,1,0:T(8,128)S(1)}, f32[1,512,2048]{2,1,0:T(8,128)}, u32[]{:S(2)}) copy-start(f32[1,512,2048]{2,1,0:T(8,128)} %param.21) | copy-start | bytes 12582916
  456.7 15.2 %copy-start.4 = (f32[512,2048]{1,0:T(8,128)S(1)}, f32[512,2048]{1,0:T(8,128)}, u32[]{:S(2)}) copy-start(f32[512,2048]{1,0:T(8,128)} %get-tuple-element.58) | copy-start | bytes 12582916
  467.7 13.1 %collective-permute-start.7 = (bf16[2048,512]{1,0:T(8,128)(2,1)S(1)}, bf16[2048,512]{1,0:T(8,128)(2,1)}, u32[]{:S(2)}, u32[]{:S(2)}) collective-permute-start(bf16[2048,512]{1,0:T(8,128)(2,1)S(1)} %get-tuple-element.64), channel_id=1, source_target_pairs={{0,1},{1,0},{2,3},{3,2},{4,5},{5,4},{6,7},{7,6}} | collective-permute-start | bytes 6291464 | tf_op jit(solution)/shard_map/ppermute | solution.py:554
  471.8 8.4 %copy-start.8 = (s32[16,1024]{1,0:T(8,128)S(1)}, s32[16,1024]{1,0:T(8,128)}, u32[]{:S(2)}) copy-start(s32[16,1024]{1,0:T(8,128)} %param.32) | copy-start | bytes 196612
  480.2 4.5 collective-permute-start.6
  711.2 68.3 %all-gather.17.cloned.1.call-start = ((), (), s32[]{:S(2)}) async-start(), calls=%async_computation.7 | async-start | bytes 12582912 | tf_op jit(solution)/shard_map/all_gather | solution.py:641
Sparse Core Ops, SparseCore 0:
  24.6 33.6 all-gather.6
  60.1 49.4 all-gather.8
  183.0 62.2 reduce-scatter.1
  247.6 30.7 all-gather.10
  280.6 194.3 all-gather.12
  711.3 18.4 all-gather.14
  761.1 18.4 all-gather.16

commit v4 on v3

--- a/solution.py
+++ b/solution.py
@@ -342,12 +342,11 @@
     )(blocks, starts, ids, low, g_rows)
 
 
-def adam_kernel(low_scale, n_wide, n_red, start_ref, stage_ref, clip_ref, ids_ref, low_ref, gw_ref, go_ref, gf_ref,
-                w_ref, m_ref, v_ref, w_out, m_out, v_out, acc_ref):
-    j = pl.program_id(0)
-    own = n_wide + n_red * stage_ref[0]
-    is_own = (j >= own) & (j < own + n_red)
-
+def adam_kernel(low_scale, first_block, n_red, start_ref, stage_ref, clip_ref, ids_ref, low_ref, *refs):
+    g_refs = refs[:1 if n_red is None else 2]
+    w_ref, m_ref, v_ref = refs[len(g_refs):len(g_refs) + 3]
+    w_out, m_out, v_out, acc_ref = refs[-4:]
+    j = first_block + pl.program_id(0)
     rows = j * ADAM_TILE + lax.broadcasted_iota(jnp.int32, (ADAM_TILE, 1), 0)
     per = ADAM_TILE // TILE
     first = jnp.minimum(start_ref[per * j] // SEG, ids_ref.shape[0] - 1)
@@ -356,17 +355,18 @@
         pick = jnp.where(rows == ids_ref[pl.ds(c, 1), :], 1.0, 0.0).astype(jnp.bfloat16)
         return low_scale * jnp.dot(pick, low_ref[pl.ds(pl.multiple_of(c * SEG, SEG), SEG), :], preferred_element_type=jnp.float32)
 
-    @pl.when(j < n_wide)
-    def _():
-        acc_ref[...] = gw_ref[...] + segment(first)
-
-    @pl.when(is_own)
-    def _():
-        acc_ref[...] = go_ref[...] + segment(first)
-
-    @pl.when((j >= n_wide) & jnp.logical_not(is_own))
-    def _():
-        acc_ref[...] = gf_ref[...] + segment(first)
+    if n_red is None:
+        acc_ref[...] = g_refs[0][...] + segment(first)
+    else:
+        is_own = pl.program_id(0) // n_red == stage_ref[0]
+
+        @pl.when(is_own)
+        def _():
+            acc_ref[...] = g_refs[0][...] + segment(first)
+
+        @pl.when(jnp.logical_not(is_own))
+        def _():
+            acc_ref[...] = g_refs[1][...] + segment(first)
 
     def add(c, _):
         acc_ref[...] += segment(c)
@@ -385,30 +385,31 @@
     lax.fori_loop(0, ADAM_TILE // 32, part, 0)
 
 
-def embed_adam(starts, stage, clip, ids, low, g_wide, g_own, g_far, embed_table, mom, vel, low_scale):
+def embed_adam(first_block, n_blocks, grads, starts, stage, clip, ids, low, embed_table, mom, vel, low_scale, held=()):
     vocab, d_model = embed_table.shape
-    n_wide, n_red = g_wide.shape[0] // ADAM_TILE, g_own.shape[0] // ADAM_TILE
-    spec = pl.BlockSpec((ADAM_TILE, d_model), lambda j, s, t, c: (j, 0))
+    n_red = n_blocks // 2 if len(grads) == 2 else None
+    spec = pl.BlockSpec((ADAM_TILE, d_model), lambda j, s, t, c: (first_block + j, 0))
     shape = jax.ShapeDtypeStruct((vocab, d_model), jnp.float32)
 
-    def held(first):
-        return pl.BlockSpec((ADAM_TILE, d_model), lambda j, s, t, c: (jnp.clip(j - n_wide - n_red * first(t[0]), 0, n_red - 1), 0))
-
-    return pl.pallas_call(
-        functools.partial(adam_kernel, low_scale, n_wide, n_red),
+    def half(first):
+        return pl.BlockSpec((ADAM_TILE, d_model), lambda j, s, t, c: (jnp.clip(j - n_red * first(t[0]), 0, n_red - 1), 0))
+
+    g_specs = [half(lambda t: t), half(lambda t: 1 - t)] if n_red else [pl.BlockSpec((ADAM_TILE, d_model), lambda j, s, t, c: (j, 0))]
+    return pl.pallas_call(
+        functools.partial(adam_kernel, low_scale, first_block, n_red),
         out_shape=[shape] * 3,
         grid_spec=pltpu.PrefetchScalarGridSpec(
-            num_scalar_prefetch=3, grid=(pl.cdiv(vocab, ADAM_TILE),),
+            num_scalar_prefetch=3, grid=(n_blocks,),
             in_specs=[pl.BlockSpec(ids.shape, lambda j, s, t, c: (0, 0)),
-                      pl.BlockSpec(low.shape, lambda j, s, t, c: (0, 0)),
-                      pl.BlockSpec((ADAM_TILE, d_model), lambda j, s, t, c: (jnp.minimum(j, n_wide - 1), 0)),
-                      held(lambda t: t), held(lambda t: 1 - t), spec, spec, spec],
+                      pl.BlockSpec(low.shape, lambda j, s, t, c: (0, 0))] + g_specs + [spec] * 3 + [pl.BlockSpec(memory_space=pl.ANY)] * len(held),
             out_specs=[spec] * 3,
             scratch_shapes=[pltpu.VMEM((ADAM_TILE, d_model), jnp.float32)]),
+        input_output_aliases={8 + len(grads) + i: i for i in range(len(held))},
         compiler_params=params(),
-        cost_estimate=pl.CostEstimate(flops=20 * vocab * d_model, bytes_accessed=28 * vocab * d_model, transcendentals=0),
+        cost_estimate=pl.CostEstimate(flops=20 * n_blocks * ADAM_TILE * d_model, bytes_accessed=28 * n_blocks * ADAM_TILE * d_model,
+                                      transcendentals=0),
         name='embed_adam',
-    )(starts, stage, clip, ids, low, g_wide, g_own, g_far, embed_table, mom, vel)
+    )(starts, stage, clip, ids, low, *grads, embed_table, mom, vel, *held)
 
 
 def next_kernel(scale, n_blocks, ids_ref, table_ref, wi0_ref, wo0_ref, wi1_ref, wo1_ref, out_ref, rows_ref, x_ref, acc_ref, sems):
@@ -626,8 +627,10 @@
         clip_scale = jnp.minimum(1.0, max_norm[0] / (jnp.sqrt(total_sq) + CLIP_EPS))
         new_first, new_mom_first, new_vel_first = adamw_update(w_first[0], mom_first[0], vel_first[0], full_first, clip_scale)
         new_second, new_mom_second, new_vel_second = adamw_update(w_second[0], mom_second[0], vel_second[0], full_second, clip_scale)
-        new_embed, new_mom_embed, new_vel_embed = embed_adam(
-            starts, blocks(stage_id), clip_scale.reshape(1), sorted_ids, low, g_wide, g_own, g_far, embed_table, mom_embed, vel_embed, low_scale)
+        n_first = rest0 * TILE // ADAM_TILE
+        update = (starts, blocks(stage_id), clip_scale.reshape(1), sorted_ids, low, embed_table, mom_embed, vel_embed, low_scale)
+        rest_rows = embed_adam(n_first, -(-vocab // ADAM_TILE) - n_first, (g_own, g_far), *update)
+        new_embed, new_mom_embed, new_vel_embed = embed_adam(0, n_first, (g_wide,), *update, held=tuple(rest_rows))
 
         next_in, next_out = new_first.astype(jnp.bfloat16), new_second.astype(jnp.bfloat16)
         next_in0, next_in1 = by_stage(next_in, other(next_in))

time: 806 us -> 808 us (level)
    pallas_call x1 -> x2, Pallas kernels: 172 us -> 174 us  [embed_adam(): pl.pallas_call(functools.partial(adam_kernel, low_scale, first_block, n_r...]
  transfers between devices with their start and end apart: 15 -> 15, of which waited for: 6 -> 6; matrix products, arithmetic and copies ran while one was open for 14% -> 14% of each run, Pallas kernels for 36% -> 44%
where the time goes in v4:
time: 808 us; the launch traced here: 802 us
  Pallas kernels  586 us (73%)
  other arithmetic  110 us (14%)
  waiting for transfers between devices  42 us (5%)
  matrix products  19.8 us (2%)
  between operations  18.2 us (2%)
  local copies, waits for them, and re-layouts  13.4 us (2%)
  blocking collectives  10 us (1%)
    pallas_call x2, Pallas kernels, embed_adam(): pl.pallas_call(functools.partial(adam_kernel, low_scale, first_block, n_r...  174 us
    pallas_call x2, Pallas kernels, next_forward(): pl.pallas_call(functools.partial(next_kernel, scale, n_tok // TOKEN_BLOCK...  99.5 us
    pallas_call x2, Pallas kernels, block_backward(): pl.pallas_call(functools.partial(backward_kernel, n_chunks, n_ff, n_rep),...  92.6 us
    pallas_call x2, Pallas kernels, head_rows(): pl.pallas_call(kernel, out_shape=jax.ShapeDtypeStruct((n_own * TILE, d_mo...  77.9 us
    pallas_call x1, Pallas kernels, head_grads(): pl.pallas_call(functools.partial(head_kernel, vocab, n_chunks, n_rep, n_o...  73.3 us
    pallas_call x1, Pallas kernels, head_stats(): pl.pallas_call(functools.partial(stats_kernel, vocab, n_tok // CHUNK, n_o...  35.1 us
    select_n x5, other arithmetic, by_stage(): return (jnp.where(low_core, own, far), jnp.where(low_core, far, own))  22.4 us
    reduce_sum x1, other arithmetic, local_step(): rank = jnp.sum(before.astype(jnp.int32), axis=1)  19.7 us
  transfers between devices with their start and end apart: 15, of which 6 were waited for; matrix products, arithmetic and copies ran while one was open for 14% of the time, Pallas kernels for 44%

profile of v4, /device:TPU:0, one launch (start us, length us, event | category | flops | bytes accessed | tf_op | source)
XLA Modules:
  0.0 802.3 jit_solution(706822066689205695)
XLA Ops:
  7.2 2.5 bitcast_convert_fusion
  9.8 7.9 add_convert_fusion
  17.7 1.1 slice.30
  18.8 1.3 collective-permute-start
  20.1 2.5 collective-permute-done
  22.6 1.9 slice_select_fusion
  24.6 10.0 %all_gather.22 = s32[2,4096]{1,0:T(2,128)S(1)} all-gather(s32[2,1024]{1,0:T(2,128)S(1)} %pad_add_fusion), channel_id=1, replica_groups=mesh['data'=4,'stage'=2] {'data'}, dimensions={1}, use_global_device_ids=true | all-gather | bytes 40960 | tf_op jit(solution)/shard_map/all_gather | solution.py:567
  35.3 0.8 convert_reduce_fusion.1.start_ref
  36.1 19.7 %convert_reduce_fusion = s32[4096]{0:T(1024)S(1)} fusion(s32[4096]{0:T(1024)S(1)} %bitcast.101), kind=kLoop, calls=%fused_computation.2 | loop fusion | flops 117436416 | bytes 32768 | tf_op jit(solution)/shard_map/reduce_sum | solution.py:575
  55.8 2.5 all-gather.7.cloned.1.call-done.z_ref
  59.2 35.1 %head_stats.1.x_ref = f32[2,4096]{1,0:T(2,128)} custom-call(s32[2]{0:T(128)} %pad_add_fusion.2.blk_ref, bf16[4096,512]{1,0:T(8,128)(2,1)} %all-gather.7.cloned.1.call-done.z_ref, f32[32128,512]{1,0:T(8,128)} %refs_1_.1), custom_call_target="tpu_custom_call" | custom-call | flops 17179869184 | bytes 8388608 | tf_op jit(solution)/shard_map/head_stats/pallas_call | solution.py:193
  94.3 10.1 %share_stats.1.norm_ref = f32[2,4096]{1,0:T(2,128)} custom-call(f32[2,4096]{1,0:T(2,128)} %head_stats.1.x_ref), custom_call_target="tpu_custom_call" | custom-call | tf_op jit(solution)/shard_map/share_stats/pallas_call | solution.py:518
  104.3 5.2 all-gather.9.cloned.1.call-done
  109.5 73.3 %head_grads.1 = (f32[2560,512]{1,0:T(8,128)}, f32[8,512,512]{2,1,0:T(8,128)}) custom-call(s32[2]{0:T(128)} %pad_add_fusion.2.blk_ref, bf16[4096,512]{1,0:T(8,128)(2,1)} %all-gather.7.cloned.1.call-done.z_ref, f32[2,4096]{1,0:T(2,128)} %share_stats.1.norm_ref, s32[1,4096]{1,0:T(1,128)} %get-tuple-element.90.tgt_ref, f32[32128,512]{1,0:T(8,128)} %refs_1_.1, ...), custom_call_target="tpu_custom_call" | custom-call | flops 51539607552 | bytes 25165824 | tf_op jit(solution)/shard_map/head_grads/pallas_call | solution.py:286
  183.5 56.2 %head_rows.2.rest_0_ = f32[6144,512]{1,0:T(8,128)} custom-call(s32[2]{0:T(128)} %pad_add_fusion.3.blk_ref, bf16[4096,512]{1,0:T(8,128)(2,1)} %all-gather.7.cloned.1.call-done.z_ref, f32[2,4096]{1,0:T(2,128)} %share_stats.1.norm_ref, s32[1,4096]{1,0:T(1,128)} %get-tuple-element.90.tgt_ref, f32[32128,512]{1,0:T(8,128)} %refs_1_.1, f32[32128,512]{1,0:T(8,128)} %g_ref.5), custom_call_target="tpu_custom_call" | custom-call | flops 38654705664 | bytes 28311552 | tf_op jit(solution)/shard_map/head_rows/pallas_call | solution.py:259
  239.7 5.6 reduce-scatter.2.cloned.1.call-done
  245.2 2.1 convert_bitcast_fusion
  248.0 3.8 bitcast_convert_fusion.1
  252.3 3.0 constant_dynamic-slice_fusion
  256.0 5.3 broadcast_select_fusion.6
  261.4 4.2 broadcast_select_fusion.2
  265.6 4.4 broadcast_select_fusion.7
  270.0 10.4 %select_reduce_fusion = s32[4096]{0:T(1024)S(1)} fusion(s32[4096]{0:T(1024)S(1)} %bitcast.102, s32[4096]{0:T(1024)S(1)} %convert_reduce_fusion), kind=kLoop, calls=%fused_computation | loop fusion | flops 50327552 | bytes 49152 | tf_op jit(solution)/shard_map/reduce_sum | solution.py:602
  281.0 21.7 %head_rows.3.g_ref.refs_0_ = f32[6144,512]{1,0:T(8,128)} custom-call(s32[2]{0:T(128)} %broadcast_add_fusion.blk_ref, bf16[4096,512]{1,0:T(8,128)(2,1)} %all-gather.7.cloned.1.call-done.z_ref, f32[2,4096]{1,0:T(2,128)} %share_stats.1.norm_ref, s32[1,4096]{1,0:T(1,128)} %get-tuple-element.90.tgt_ref, ...), custom_call_target="tpu_custom_call", output_to_operand_aliasing={{}: (6, {})} | custom-call | flops 12884901888 | bytes 9437184 | tf_op jit(solution)/shard_map/head_rows/pallas_call | solution.py:259
  303.2 3.0 constant_dynamic-slice_fusion.1.g_ref
  306.2 46.1 %block_backward.2 = (bf16[2048,512]{1,0:T(8,128)(2,1)}, f32[512,2048]{1,0:T(8,128)}, f32[2048,512]{1,0:T(8,128)}, f32[8,512]{1,0:T(8,128)}) custom-call(bf16[2048,512]{1,0:T(8,128)(2,1)} %constant_dynamic-slice_fusion.1.g_ref, bf16[2048,512]{1,0:T(8,128)(2,1)} %get-tuple-element.79.x_ref, bf16[512,2048]{1,0:T(8,128)(2,1)} %get-tuple-element.87.wi_ref, ...), custom_call_target="tpu_custom_call" | custom-call | flops 21474836480 | bytes 12582912 | tf_op jit(solution)/shard_map/block_backward/pallas_call | solution.py:123
  352.4 46.4 %block_backward.3 = (bf16[2048,512]{1,0:T(8,128)(2,1)}, f32[512,2048]{1,0:T(8,128)}, f32[2048,512]{1,0:T(8,128)}, f32[8,512]{1,0:T(8,128)}) custom-call(bf16[2048,512]{1,0:T(8,128)(2,1)} %get-tuple-element.54.g_ref, bf16[2048,512]{1,0:T(8,128)(2,1)} %get-tuple-element.78.x_ref, bf16[512,2048]{1,0:T(8,128)(2,1)} %get-tuple-element.86.wi_ref, ...), custom_call_target="tpu_custom_call" | custom-call | flops 21474836480 | bytes 12582912 | tf_op jit(solution)/shard_map/block_backward/pallas_call | solution.py:123
  398.9 11.9 %fusion.12 = bf16[4096,512]{1,0:T(8,128)(2,1)} fusion(bf16[2048,512]{1,0:T(8,128)(2,1)} %get-tuple-element.55, s32[2048]{0:T(1024)S(1)} %dynamic-slice-done), kind=kOutput, calls=%fused_computation.21 | convolution fusion | flops 8600420352 | bytes 6299648 | tf_op jit(solution)/shard_map/dot_general | solution.py:614
  413.4 7.1 collective-permute-done.4
  420.5 6.7 add.92.low_ref
  427.2 7.6 rows_sumsq.3
  434.8 9.7 %rows_sumsq.2 = f32[8,512]{1,0:T(8,128)} custom-call(s32[2]{0:T(128)} %get-tuple-element.92.blk_ref, s32[65]{0:T(128)} %convert_reduce_fusion.1.start_ref, s32[16,256]{1,0:T(8,128)} %reshape.53.ids_ref, bf16[4096,512]{1,0:T(8,128)(2,1)} %add.92.low_ref, f32[2560,512]{1,0:T(8,128)} %get-tuple-element.56.g_ref), custom_call_target="tpu_custom_call" | custom-call | tf_op jit(solution)/shard_map/rows_sumsq/pallas_call | solution.py:331
  445.1 1.3 reduce_sum.66
  448.3 6.0 share_sums.1
  454.4 1.4 slice_reduce_fusion
  456.5 11.1 %fusion.38 = (bf16[2048,512]{1,0:T(8,128)(2,1)S(1)}, f32[2048,512]{1,0:T(8,128)}, f32[2048,512]{1,0:T(8,128)}, f32[2048,512]{1,0:T(8,128)}) fusion(f32[1,2048,512]{2,1,0:T(8,128)} %param.18, f32[2048,512]{1,0:T(8,128)} %get-tuple-element.62, f32[2048,512]{1,0:T(8,128)} %get-tuple-element.63, pred[]{:T(512)S(6)} %eq.14, f32[]{:T(128)} %min.3, ...), kind=kLoop, calls=%fused_computation.76 | loop fusion | flops 18874368 | bytes 35651588 | tf_op jit(solution)/shard_map/convert_element_type | solution.py:635
  468.0 1.3 copy-done.2
  469.3 1.2 copy-done.3
  470.5 1.2 copy-done.4
  471.7 8.4 %fusion.40 = (bf16[512,2048]{1,0:T(8,128)(2,1)}, f32[512,2048]{1,0:T(8,128)}, f32[512,2048]{1,0:T(8,128)}, f32[512,2048]{1,0:T(8,128)}) fusion(f32[1,512,2048]{2,1,0:T(8,128)S(1)} %copy-done.1, f32[512,2048]{1,0:T(8,128)} %get-tuple-element.60, f32[512,2048]{1,0:T(8,128)S(1)} %copy-done.4, pred[]{:T(512)S(6)} %eq.14, f32[]{:T(128)} %min.3, ...), kind=kLoop, calls=%fused_computation.77 | loop fusion | flops 18874368 | bytes 35651588 | tf_op jit(solution)/shard_map/convert_element_type | solution.py:635
  480.7 3.9 broadcast_select_fusion.4
  484.5 4.5 broadcast_select_fusion
  489.1 64.9 %embed_adam.2 = (f32[32128,512]{1,0:T(8,128)}, f32[32128,512]{1,0:T(8,128)}, f32[32128,512]{1,0:T(8,128)}) custom-call(s32[65]{0:T(128)} %convert_reduce_fusion.1.start_ref, s32[1]{0:T(128)} %bitcast.26.stage_ref, f32[1]{0:T(128)} %bitcast.27.clip_ref, s32[16,256]{1,0:T(8,128)} %reshape.53.ids_ref, bf16[4096,512]{1,0:T(8,128)(2,1)} %add.92.low_ref, ...), custom_call_target="tpu_custom_call" | custom-call | flops 125829120 | bytes 176160768 | tf_op jit(solution)/shard_map/embed_adam/pallas_call | solution.py:398
  554.0 109.1 %embed_adam.3 = (f32[32128,512]{1,0:T(8,128)}, f32[32128,512]{1,0:T(8,128)}, f32[32128,512]{1,0:T(8,128)}) custom-call(s32[65]{0:T(128)} %convert_reduce_fusion.1.start_ref, s32[1]{0:T(128)} %bitcast.26.stage_ref, f32[1]{0:T(128)} %bitcast.27.clip_ref, s32[16,256]{1,0:T(8,128)} %reshape.53.ids_ref, ...), custom_call_target="tpu_custom_call", output_to_operand_aliasing={{0}: (9, {}), {1}: (10, {}), {2}: (11, {})} | custom-call | flops 209715200 | bytes 293601280 | tf_op jit(solution)/shard_map/embed_adam/pallas_call | solution.py:398
  663.1 49.9 %next_forward.2 = bf16[4096,512]{1,0:T(8,128)(2,1)} custom-call(s32[4096]{0:T(1024)} %get-tuple-element.95.ids_ref, f32[32128,512]{1,0:T(8,128)} %get-tuple-element.36.table_ref, bf16[512,2048]{1,0:T(8,128)(2,1)} %get-tuple-element.83.wi0_ref, bf16[2048,512]{1,0:T(8,128)(2,1)} %get-tuple-element.81.wo0_ref, bf16[512,2048]{1,0:T(8,128)(2,1)} %get-tuple-element.82.wi1_ref, ...), custom_call_target="tpu_custom_call" | custom-call | flops 34359738368 | bytes 12582912 | tf_op jit(solution)/shard_map/next_forward/pallas_call | solution.py:460
  713.1 49.6 %next_forward.3 = bf16[4096,512]{1,0:T(8,128)(2,1)} custom-call(s32[4096]{0:T(1024)} %get-tuple-element.94.ids_ref, f32[32128,512]{1,0:T(8,128)} %get-tuple-element.36.table_ref, bf16[512,2048]{1,0:T(8,128)(2,1)} %get-tuple-element.83.wi0_ref, bf16[2048,512]{1,0:T(8,128)(2,1)} %get-tuple-element.81.wo0_ref, bf16[512,2048]{1,0:T(8,128)(2,1)} %get-tuple-element.82.wi1_ref, ...), custom_call_target="tpu_custom_call" | custom-call | flops 34359738368 | bytes 12582912 | tf_op jit(solution)/shard_map/next_forward/pallas_call | solution.py:460
  762.7 18.5 %all-gather.17.cloned.1.call-done = bf16[2,4,1024,512]{3,2,1,0:T(8,128)(2,1)} async-done(((bf16[1,4,1024,512]{3,2,1,0:T(8,128)(2,1)}), bf16[2,4,1024,512]{3,2,1,0:T(8,128)(2,1)}) %all-gather.17.cloned.1.call-update) | async-done | bytes 8388624 | tf_op jit(solution)/shard_map/all_gather | solution.py:644
  781.2 13.8 %pad_maximum_fusion = bf16[2,2,4,1024,512]{4,3,2,1,0:T(8,128)(2,1)} fusion(bf16[2,1,4,1024,512]{4,3,2,1,0:T(8,128)(2,1)} %bitcast.90, bf16[2,1,4,1024,512]{4,3,2,1,0:T(8,128)(2,1)} %bitcast.89), kind=kLoop, calls=%fused_computation.8 | loop fusion | flops 8388608 | bytes 33554432 | tf_op jit(solution)/shard_map/stack | solution.py:645
  (70 shorter events, 8.8 us)
Async XLA Ops:
  7.2 2.6 copy-start.6
  7.2 51.1 %all-gather.7.cloned.1.call-start = ((), (), s32[]{:S(2)}) async-start(), calls=%async_computation.1 | async-start | bytes 4718592 | tf_op jit(solution)/shard_map/all_gather | solution.py:571
  9.8 14.8 %copy-start.12 = (s32[1024]{0:T(1024)S(1)}, s32[1024]{0:T(1024)}, u32[]{:S(2)}) copy-start(s32[1024]{0:T(1024)} %param.31) | copy-start | bytes 12292
  9.8 14.8 %copy-start.13 = (s32[1024]{0:T(1024)S(1)}, s32[1024]{0:T(1024)}, u32[]{:S(2)}) copy-start(s32[1024]{0:T(1024)} %param.30) | copy-start | bytes 12292
  18.8 3.8 collective-permute-start
  24.5 85.0 %all-gather.9.cloned.1.call-start = ((), (), s32[]{:S(2)}) async-start(), calls=%async_computation.2 | async-start | bytes 5242880 | tf_op jit(solution)/shard_map/all_gather | solution.py:580
  55.8 214.3 %copy-start.11 = (s32[4096]{0:T(1024)}, s32[4096]{0:T(1024)S(1)}, u32[]{:S(2)}) copy-start(s32[4096]{0:T(1024)S(1)} %convert_reduce_fusion) | copy-start | bytes 49156
  58.3 186.9 %reduce-scatter.2.cloned.1.call-start = ((), (), s32[]{:S(2)}) async-start(), calls=%async_computation.3 | async-start | bytes 9437184 | tf_op jit(solution)/shard_map/reduce_scatter | solution.py:593
  182.8 119.9 %all-gather.11.cloned.1.call-start = ((), (), s32[]{:S(2)}) async-start(), calls=%async_computation.4 | async-start | bytes 4718592 | tf_op jit(solution)/shard_map/all_gather | solution.py:601
  247.4 306.6 %all-gather.13.cloned.1.call-start = ((), (), s32[]{:S(2)}) async-start(), calls=%async_computation.5 | async-start | bytes 47185920 | tf_op jit(solution)/shard_map/all_gather | solution.py:606
  247.9 514.8 %all-gather.15.cloned.1.call-start = ((), (), s32[]{:S(2)}) async-start(), calls=%async_computation.6 | async-start | bytes 12582912 | tf_op jit(solution)/shard_map/all_gather | solution.py:644
  248.0 8.0 collective-permute-start.3
  251.9 9.5 %collective-permute-start.2 = (bf16[512,2048]{1,0:T(8,128)(2,1)}, bf16[512,2048]{1,0:T(8,128)(2,1)}, u32[]{:S(2)}, u32[]{:S(2)}) collective-permute-start(bf16[512,2048]{1,0:T(8,128)(2,1)} %bitcast_convert_fusion.1), channel_id=1, source_target_pairs={{0,1},{1,0},{2,3},{3,2},{4,5},{5,4},{6,7},{7,6}} | collective-permute-start | bytes 6291464 | tf_op jit(solution)/shard_map/ppermute | solution.py:555
  255.4 10.2 %collective-permute-start.1 = (bf16[2048,512]{1,0:T(8,128)(2,1)}, bf16[2048,512]{1,0:T(8,128)(2,1)}, u32[]{:S(2)}, u32[]{:S(2)}) collective-permute-start(bf16[2048,512]{1,0:T(8,128)(2,1)} %constant_dynamic-slice_fusion), channel_id=1, source_target_pairs={{0,1},{1,0},{2,3},{3,2},{4,5},{5,4},{6,7},{7,6}} | collective-permute-start | bytes 6291464 | tf_op jit(solution)/shard_map/ppermute | solution.py:555
  256.0 5.4 copy-start
  261.3 4.3 copy-start.5
  302.7 186.4 %collective-permute-start.5 = (f32[6144,512]{1,0:T(8,128)}, f32[6144,512]{1,0:T(8,128)}, u32[]{:S(2)}, u32[]{:S(2)}) collective-permute-start(f32[6144,512]{1,0:T(8,128)} %head_rows.3.g_ref.refs_0_), channel_id=1, source_target_pairs={{0,1},{1,0},{2,3},{3,2},{4,5},{5,4},{6,7},{7,6}} | collective-permute-start | bytes 37748744 | tf_op jit(solution)/shard_map/ppermute | solution.py:555
  352.4 46.5 %dynamic-slice-start = ((s32[4096]{0:T(1024)}, s32[]{:T(128)}), s32[2048]{0:T(1024)S(1)}, s32[]{:S(2)}) async-start(s32[4096]{0:T(1024)} %copy-done.11, s32[]{:T(128)} %select_n.94), calls=%async_computation.8 | async-start | bytes 16896 | tf_op jit(solution)/shard_map/dynamic_slice | solution.py:612
  398.8 13.3 %copy-start.9 = (f32[8,512]{1,0:T(8,128)S(1)}, f32[8,512]{1,0:T(8,128)}, u32[]{:S(2)}) copy-start(f32[8,512]{1,0:T(8,128)} %get-tuple-element.59) | copy-start | bytes 49156
  398.8 13.3 %copy-start.10 = (f32[8,512]{1,0:T(8,128)S(1)}, f32[8,512]{1,0:T(8,128)}, u32[]{:S(2)}) copy-start(f32[8,512]{1,0:T(8,128)} %get-tuple-element.58) | copy-start | bytes 49156
  410.8 9.7 %collective-permute-start.4 = (bf16[4096,512]{1,0:T(8,128)(2,1)}, bf16[4096,512]{1,0:T(8,128)(2,1)}, u32[]{:S(2)}, u32[]{:S(2)}) collective-permute-start(bf16[4096,512]{1,0:T(8,128)(2,1)} %fusion.12), channel_id=1, source_target_pairs={{0,1},{1,0},{2,3},{3,2},{4,5},{5,4},{6,7},{7,6}} | collective-permute-start | bytes 12582920 | tf_op jit(solution)/shard_map/ppermute | solution.py:555
  434.8 9.7 %copy-start.7 = (f32[8,512]{1,0:T(8,128)S(1)}, f32[8,512]{1,0:T(8,128)}, u32[]{:S(2)}) copy-start(f32[8,512]{1,0:T(8,128)} %rows_sumsq.3) | copy-start | bytes 49156
  456.5 11.5 %copy-start.1 = (f32[1,512,2048]{2,1,0:T(8,128)S(1)}, f32[1,512,2048]{2,1,0:T(8,128)}, u32[]{:S(2)}) copy-start(f32[1,512,2048]{2,1,0:T(8,128)} %param.17) | copy-start | bytes 12582916
  456.5 12.8 %copy-start.2 = (f32[1,512,2048]{2,1,0:T(8,128)S(1)}, f32[1,512,2048]{2,1,0:T(8,128)}, u32[]{:S(2)}) copy-start(f32[1,512,2048]{2,1,0:T(8,128)} %param.19) | copy-start | bytes 12582916
  456.5 14.0 %copy-start.3 = (f32[1,512,2048]{2,1,0:T(8,128)S(1)}, f32[1,512,2048]{2,1,0:T(8,128)}, u32[]{:S(2)}) copy-start(f32[1,512,2048]{2,1,0:T(8,128)} %param.21) | copy-start | bytes 12582916
  456.5 15.2 %copy-start.4 = (f32[512,2048]{1,0:T(8,128)S(1)}, f32[512,2048]{1,0:T(8,128)}, u32[]{:S(2)}) copy-start(f32[512,2048]{1,0:T(8,128)} %get-tuple-element.61) | copy-start | bytes 12582916
  467.6 13.1 %collective-permute-start.7 = (bf16[2048,512]{1,0:T(8,128)(2,1)S(1)}, bf16[2048,512]{1,0:T(8,128)(2,1)}, u32[]{:S(2)}, u32[]{:S(2)}) collective-permute-start(bf16[2048,512]{1,0:T(8,128)(2,1)S(1)} %get-tuple-element.70), channel_id=1, source_target_pairs={{0,1},{1,0},{2,3},{3,2},{4,5},{5,4},{6,7},{7,6}} | collective-permute-start | bytes 6291464 | tf_op jit(solution)/shard_map/ppermute | solution.py:555
  471.7 8.4 %copy-start.8 = (s32[16,1024]{1,0:T(8,128)S(1)}, s32[16,1024]{1,0:T(8,128)}, u32[]{:S(2)}) copy-start(s32[16,1024]{1,0:T(8,128)} %param.32) | copy-start | bytes 196612
  480.0 4.5 collective-permute-start.6
  713.0 68.2 %all-gather.17.cloned.1.call-start = ((), (), s32[]{:S(2)}) async-start(), calls=%async_computation.7 | async-start | bytes 12582912 | tf_op jit(solution)/shard_map/all_gather | solution.py:644
Sparse Core Ops, SparseCore 0:
  24.6 33.5 all-gather.6
  60.1 49.4 all-gather.8
  183.0 62.2 reduce-scatter.1
  247.5 30.7 all-gather.10
  280.0 194.6 all-gather.12
  713.1 18.3 all-gather.14
  762.8 18.3 all-gather.16
